TPU v7x, 256 devices: a whole 4x4x8 slice. The times are simulated.
256 devices in a mesh: row: 16 (over y_lo, x, core), col: 16 (over y_hi, z).
Axes of the slice: x: 4, y: 4 (y_hi: 2, y_lo: 2; y = y_hi * 2 + y_lo), z: 8, core: 2. Of those that a mesh axis runs over, the one named last changes fastest.
Arguments:
- objects: float32 [4, 8192, 8192], P(None, 'row', 'col'), may hold values from -1 to 1, as said below
- probe: float32 [2, 256, 256], replicated, may hold values from -6 to 6
- kernel: float32 [2, 256, 256], replicated, may hold values from -1 to 1, as said below
- measured: float32 [16, 16, 9, 256, 256], P('row', 'col'), may hold values from 0.3 to 3
- offsets: int32 [16, 16, 9, 2], P('row', 'col'), may hold values from -64 to 320, as said below
Outputs:
- updated: float32 [4, 8192, 8192], P(None, 'row', 'col')
Inputs may be any that keep to these rules, and one draw needn't show every extreme that they name: Every window lies inside the object: tiles in the first row or column have offsets of 0 or more there, tiles in the last have offsets of at most 256 there. `objects`: real and imaginary parts of each slice give a magnitude between 0.6 and 1. `kernel`: each entry has magnitude 1.
All inputs are finite; a program needn't handle non-finite values.
Results may differ from a plain program's by a relative error of at most 0.012.
Values sent between devices are 32-bit elements; how exact they have to be, the bound alone decides.
A program may use at most 128 MiB of HBM per device.

v0:
```python
import jax
import jax.numpy as jnp
from jax import lax
from jax.sharding import PartitionSpec as P

HALO = 64


RATE = 0.5


def padded_2(x, sides, width):
    for axis, dim in sides:
        devices, length = (lax.axis_size(axis), x.shape[dim])
        up = [(i, (i + 1) % devices) for i in range(devices - 1)]
        down = [(j, i) for i, j in up]
        last = lax.slice_in_dim(x, length - width, length, axis=dim)
        initial = lax.slice_in_dim(x, 0, width, axis=dim)
        before = lax.ppermute(last, axis, up)
        after = lax.ppermute(initial, axis, down)
        x = jnp.concatenate([before, x, after], axis=dim)
    return x


def make_tables(width):
    index = jnp.arange(width, dtype=jnp.int32)
    product = index[:, None] * index[None, :] % width
    angle = 2.0 * jnp.pi / width * product.astype(jnp.float32)
    norm = 1.0 / jnp.sqrt(jnp.float32(width))
    cosine = jnp.cos(angle) * norm
    sine = jnp.sin(angle) * norm

    def blocks(real_part, imag_part):
        left = jnp.concatenate(
            [
                jnp.concatenate([real_part, -imag_part], 1),
                jnp.concatenate([imag_part, real_part], 1),
            ],
            0,
        )
        right = jnp.concatenate(
            [
                jnp.concatenate([real_part, imag_part], 1),
                jnp.concatenate([-imag_part, real_part], 1),
            ],
            0,
        )
        return (left.astype(jnp.bfloat16), right.astype(jnp.bfloat16))

    return (blocks(cosine, -sine), blocks(cosine, sine))


def transform(real_part, imag_part, table):
    left, right = table
    width = real_part.shape[0]
    stacked = jnp.concatenate([real_part, imag_part], 0).astype(jnp.bfloat16)
    first = jnp.dot(left, stacked, preferred_element_type=jnp.float32)
    middle = jnp.concatenate([first[:width], first[width:]], 1).astype(jnp.bfloat16)
    result = jnp.dot(middle, right, preferred_element_type=jnp.float32)
    return (result[:, :width], result[:, width:])


def position_gradient(window, probe, kernel, amplitude, tables):
    forward, inverse = tables
    o1r, o1i, o2r, o2i = (window[0], window[1], window[2], window[3])
    pr, pim = (probe[0], probe[1])
    kr, kim = (kernel[0], kernel[1])
    ar = pr * o1r - pim * o1i
    ai = pr * o1i + pim * o1r
    fr, fi = transform(ar, ai, forward)
    br = kr * fr - kim * fi
    bi = kr * fi + kim * fr
    sr, si = transform(br, bi, inverse)
    er = sr * o2r - si * o2i
    ei = sr * o2i + si * o2r
    zr, zi = transform(er, ei, forward)
    factor = 1.0 - amplitude / jnp.sqrt(zr * zr + zi * zi + 1.0)
    gr, gi = transform(zr * factor, zi * factor, inverse)
    g2r = sr * gr + si * gi
    g2i = sr * gi - si * gr
    hr = o2r * gr + o2i * gi
    hi = o2r * gi - o2i * gr
    ur, ui = transform(hr, hi, forward)
    vr = kr * ur + kim * ui
    vi = kr * ui - kim * ur
    wr, wi = transform(vr, vi, inverse)
    g1r = pr * wr + pim * wi
    g1i = pr * wi - pim * wr
    return jnp.stack([g1r, g1i, g2r, g2i])


def per_device(objects, probe, kernel, measured, offsets):
    tile = objects.shape[1]
    width = probe.shape[1]
    margin = HALO
    extent = tile + 2 * margin
    tables = make_tables(width)
    zero = jnp.zeros((), jnp.int32)
    padded = padded_2(objects, (("row", 1), ("col", 2)), margin)
    source_cols = jnp.arange(width, dtype=jnp.int32)[:, None]
    target_cols = jnp.arange(extent, dtype=jnp.int32)[None, :]

    def accumulate(which, gradient):
        top = offsets[0, 0, which, 0] + margin
        left = offsets[0, 0, which, 1] + margin
        window = lax.dynamic_slice(padded, (zero, top, left), (4, width, width))
        piece = position_gradient(window, probe, kernel, measured[0, 0, which], tables)
        placer = (source_cols + left == target_cols).astype(jnp.float32)
        spread = jnp.dot(
            piece.reshape(4 * width, width), placer, preferred_element_type=jnp.float32
        )
        spread = spread.reshape(4, width, extent)
        current = lax.dynamic_slice(gradient, (zero, top, zero), (4, width, extent))
        return lax.dynamic_update_slice(gradient, current + spread, (zero, top, zero))

    gradient = lax.fori_loop(
        0, offsets.shape[2], accumulate, jnp.zeros((4, extent, extent), jnp.float32)
    )
    cycle = padded_2(gradient, (("row", 1), ("col", 2)), margin)
    inner = gradient[:, margin : margin + tile, margin : margin + tile]
    gap_rows = jnp.zeros((4, tile - 2 * margin, tile), jnp.float32)
    gap_cols = jnp.zeros((4, tile, tile - 2 * margin), jnp.float32)
    gap_corner = jnp.zeros((4, margin, tile - 2 * margin), jnp.float32)
    top = cycle[:, :margin, 2 * margin : 2 * margin + tile]
    bottom = cycle[:, extent + margin :, 2 * margin : 2 * margin + tile]
    left = cycle[:, 2 * margin : 2 * margin + tile, :margin]
    right = cycle[:, 2 * margin : 2 * margin + tile, extent + margin :]
    corner_top = jnp.concatenate(
        [cycle[:, :margin, :margin], gap_corner, cycle[:, :margin, extent + margin :]], 2
    )
    corner_bottom = jnp.concatenate(
        [
            cycle[:, extent + margin :, :margin],
            gap_corner,
            cycle[:, extent + margin :, extent + margin :],
        ],
        2,
    )
    vertical = jnp.concatenate([top + corner_top, gap_rows, bottom + corner_bottom], 1)
    horizontal = jnp.concatenate([left, gap_cols, right], 2)
    total = inner + vertical + horizontal
    return objects - RATE * total


def solution(mesh):
    return jax.shard_map(
        per_device,
        mesh=mesh,
        in_specs=(
            P(None, "row", "col"),
            P(),
            P(),
            P("row", "col", None, None, None),
            P("row", "col", None, None),
        ),
        out_specs=P(None, "row", "col"),
        check_vma=False,
    )
```

profile of v0, /device:TPU:27, one launch (start us, length us, event | category | flops | bytes accessed | tf_op | source)
XLA Modules:
  0.0 400.8 jit_solution(17583620195655280873)
XLA Ops:
  1.3 3.7 collective-permute-start
  5.0 1.9 collective-permute-start.1
  6.9 5.2 %copy.18 = f32[4,512,512]{1,2,0:T(8,128)} copy(f32[4,512,512]{2,1,0:T(8,128)} %param.7) | data formatting | bytes 8388608 | tf_op args[0]
  12.5 3.0 collective-permute-done.1
  15.8 2.8 pad_maximum_fusion.10
  18.6 3.5 collective-permute-start.2
  22.1 6.5 %collective-permute-start.3 = (f32[4,640,64]{1,2,0:T(8,128)}, f32[4,640,64]{1,2,0:T(8,128)}, u32[]{:S(2)}, u32[]{:S(2)}) collective-permute-start(f32[4,640,64]{1,2,0:T(8,128)} %get-tuple-element.436), channel_id=1, source_target_pairs={{1,0},{2,1},{3,2},{4,3},{5,4},{6,5},{7,6},{8,7},{9,8},{10,9},{11,1... | collective-permute-start | bytes 1966088 | tf_op jit(solution)/shard_map/ppermute | solution.py:20
  31.6 9.2 %collective-permute-done.2 = f32[4,640,64]{1,2,0:T(8,128)S(1)} collective-permute-done((f32[4,640,64]{1,2,0:T(8,128)}, f32[4,640,64]{1,2,0:T(8,128)S(1)}, u32[]{:S(2)}, u32[]{:S(2)}) %collective-permute-start.2) | collective-permute-done | bytes 655392 | tf_op jit(solution)/shard_map/ppermute | solution.py:19
  40.9 1.9 collective-permute-done.3
  42.7 5.9 %pad_maximum_fusion = f32[4,640,640]{1,2,0:T(8,128)} fusion(f32[4,640,64]{1,2,0:T(8,128)} %collective-permute-done.3, f32[4,64,512]{1,2,0:T(8,128)S(1)} %copy.19, f32[4,512,512]{1,2,0:T(8,128)} %copy.18, f32[4,64,512]{1,2,0:T(8,128)S(1)} %copy.17, f32[4,640,64]{1,2,0:T(8,128)S(1)} %collective-permute-done.2), kind=kLoop, calls=%fused_computation.138 | loop fusion | flops 6553600 | bytes 13107200 | tf_op jit(solution)/shard_map/concatenate | solution.py:21
  48.6 3.2 broadcast_in_dim.16
  51.8 290.9 %while.17 = (s32[]{:T(128)}, f32[4,640,640]{2,1,0:T(8,128)}, s32[1,1,9,2]{2,3,1,0:T(2,128)S(1)}, f32[2,256,256]{2,1,0:T(8,128)}, f32[2,256,256]{2,1,0:T(8,128)},...) while((s32[]{:T(128)}, f32[4,640,640]{2,1,0:T(8,128)}, ...), condition=%wide.region_1.2_spmd.clone, body=%wide.region_0.1_spmd.clone.sunk | while | flops 1959166208 | bytes 42731852 | solution.py:116
  55.0 1.7 constant_dynamic-slice_fusion.6
  67.7 1.4 fusion.226
  73.5 2.5 dynamic-slice_add_fusion.2
  76.0 8.2 %dynamic_update_slice.13 = f32[4,640,640]{2,1,0:T(8,128)} dynamic-update-slice(f32[4,640,640]{2,1,0:T(8,128)} %get-tuple-element.589, f32[4,256,640]{2,1,0:T(8,128)S(1)} %dynamic-slice_add_fusion.2, s32[]{:T(128)} %constant.93.clone.1..sunk, s32[]{:T(128)S(6)} %select_n.72, s32[]{:T(128)} %constant.93.clone.1..sunk) | dynamic-update-slice | bytes 5242884 | tf_op jit(solution)/shard_map/while/body/eval_jaxpr/dynamic_update_slice | solution.py:114
  87.4 1.7 constant_dynamic-slice_fusion.6
  90.5 1.4 fusion.211
  95.5 1.4 fusion.219
  100.1 1.4 fusion.226
  105.9 2.5 dynamic-slice_add_fusion.2
  108.4 8.2 %dynamic_update_slice.13 = f32[4,640,640]{2,1,0:T(8,128)} dynamic-update-slice(f32[4,640,640]{2,1,0:T(8,128)} %get-tuple-element.589, f32[4,256,640]{2,1,0:T(8,128)S(1)} %dynamic-slice_add_fusion.2, s32[]{:T(128)} %constant.93.clone.1..sunk, s32[]{:T(128)S(6)} %select_n.72, s32[]{:T(128)} %constant.93.clone.1..sunk) | dynamic-update-slice | bytes 5242884 | tf_op jit(solution)/shard_map/while/body/eval_jaxpr/dynamic_update_slice | solution.py:114
  119.7 1.7 constant_dynamic-slice_fusion.6
  122.8 1.4 fusion.211
  127.8 1.4 fusion.219
  132.4 1.4 fusion.226
  138.3 2.5 dynamic-slice_add_fusion.2
  140.7 8.2 %dynamic_update_slice.13 = f32[4,640,640]{2,1,0:T(8,128)} dynamic-update-slice(f32[4,640,640]{2,1,0:T(8,128)} %get-tuple-element.589, f32[4,256,640]{2,1,0:T(8,128)S(1)} %dynamic-slice_add_fusion.2, s32[]{:T(128)} %constant.93.clone.1..sunk, s32[]{:T(128)S(6)} %select_n.72, s32[]{:T(128)} %constant.93.clone.1..sunk) | dynamic-update-slice | bytes 5242884 | tf_op jit(solution)/shard_map/while/body/eval_jaxpr/dynamic_update_slice | solution.py:114
  152.1 1.7 constant_dynamic-slice_fusion.6
  155.2 1.4 fusion.211
  160.2 1.4 fusion.219
  164.8 1.4 fusion.226
  170.6 2.5 dynamic-slice_add_fusion.2
  173.1 8.2 %dynamic_update_slice.13 = f32[4,640,640]{2,1,0:T(8,128)} dynamic-update-slice(f32[4,640,640]{2,1,0:T(8,128)} %get-tuple-element.589, f32[4,256,640]{2,1,0:T(8,128)S(1)} %dynamic-slice_add_fusion.2, s32[]{:T(128)} %constant.93.clone.1..sunk, s32[]{:T(128)S(6)} %select_n.72, s32[]{:T(128)} %constant.93.clone.1..sunk) | dynamic-update-slice | bytes 5242884 | tf_op jit(solution)/shard_map/while/body/eval_jaxpr/dynamic_update_slice | solution.py:114
  184.4 1.7 constant_dynamic-slice_fusion.6
  203.0 2.5 dynamic-slice_add_fusion.2
  205.4 8.2 %dynamic_update_slice.13 = f32[4,640,640]{2,1,0:T(8,128)} dynamic-update-slice(f32[4,640,640]{2,1,0:T(8,128)} %get-tuple-element.589, f32[4,256,640]{2,1,0:T(8,128)S(1)} %dynamic-slice_add_fusion.2, s32[]{:T(128)} %constant.93.clone.1..sunk, s32[]{:T(128)S(6)} %select_n.72, s32[]{:T(128)} %constant.93.clone.1..sunk) | dynamic-update-slice | bytes 5242884 | tf_op jit(solution)/shard_map/while/body/eval_jaxpr/dynamic_update_slice | solution.py:114
  216.8 1.7 constant_dynamic-slice_fusion.6
  229.6 1.4 fusion.226
  235.4 2.5 dynamic-slice_add_fusion.2
  237.8 8.2 %dynamic_update_slice.13 = f32[4,640,640]{2,1,0:T(8,128)} dynamic-update-slice(f32[4,640,640]{2,1,0:T(8,128)} %get-tuple-element.589, f32[4,256,640]{2,1,0:T(8,128)S(1)} %dynamic-slice_add_fusion.2, s32[]{:T(128)} %constant.93.clone.1..sunk, s32[]{:T(128)S(6)} %select_n.72, s32[]{:T(128)} %constant.93.clone.1..sunk) | dynamic-update-slice | bytes 5242884 | tf_op jit(solution)/shard_map/while/body/eval_jaxpr/dynamic_update_slice | solution.py:114
  249.2 1.7 constant_dynamic-slice_fusion.6
  261.9 1.4 fusion.226
  267.7 2.5 dynamic-slice_add_fusion.2
  270.2 8.1 %dynamic_update_slice.13 = f32[4,640,640]{2,1,0:T(8,128)} dynamic-update-slice(f32[4,640,640]{2,1,0:T(8,128)} %get-tuple-element.589, f32[4,256,640]{2,1,0:T(8,128)S(1)} %dynamic-slice_add_fusion.2, s32[]{:T(128)} %constant.93.clone.1..sunk, s32[]{:T(128)S(6)} %select_n.72, s32[]{:T(128)} %constant.93.clone.1..sunk) | dynamic-update-slice | bytes 5242884 | tf_op jit(solution)/shard_map/while/body/eval_jaxpr/dynamic_update_slice | solution.py:114
  281.5 1.7 constant_dynamic-slice_fusion.6
  289.5 1.4 fusion.219
  294.2 1.4 fusion.226
  300.0 2.5 dynamic-slice_add_fusion.2
  302.5 8.0 %dynamic_update_slice.13 = f32[4,640,640]{2,1,0:T(8,128)} dynamic-update-slice(f32[4,640,640]{2,1,0:T(8,128)} %get-tuple-element.589, f32[4,256,640]{2,1,0:T(8,128)S(1)} %dynamic-slice_add_fusion.2, s32[]{:T(128)} %constant.93.clone.1..sunk, s32[]{:T(128)S(6)} %select_n.72, s32[]{:T(128)} %constant.93.clone.1..sunk) | dynamic-update-slice | bytes 5242884 | tf_op jit(solution)/shard_map/while/body/eval_jaxpr/dynamic_update_slice | solution.py:114
  313.7 1.7 constant_dynamic-slice_fusion.6
  332.2 2.5 dynamic-slice_add_fusion.2
  334.7 8.1 %dynamic_update_slice.13 = f32[4,640,640]{2,1,0:T(8,128)} dynamic-update-slice(f32[4,640,640]{2,1,0:T(8,128)} %get-tuple-element.589, f32[4,256,640]{2,1,0:T(8,128)S(1)} %dynamic-slice_add_fusion.2, s32[]{:T(128)} %constant.93.clone.1..sunk, s32[]{:T(128)S(6)} %select_n.72, s32[]{:T(128)} %constant.93.clone.1..sunk) | dynamic-update-slice | bytes 5242884 | tf_op jit(solution)/shard_map/while/body/eval_jaxpr/dynamic_update_slice | solution.py:114
  344.1 2.8 collective-permute-start.4
  347.0 1.9 collective-permute-start.5
  348.9 8.2 %copy.22 = f32[4,640,640]{1,2,0:T(8,128)} copy(f32[4,640,640]{2,1,0:T(8,128)} %get-tuple-element.337) | data formatting | bytes 13107200 | tf_op jit(solution)/shard_map/while | solution.py:116
  359.0 1.5 copy.23
  360.5 2.7 pad_maximum_fusion.3
  363.2 2.0 collective-permute-start.6
  365.2 7.8 %collective-permute-start.7 = (f32[4,768,64]{1,2,0:T(8,128)}, f32[4,768,64]{1,2,0:T(8,128)S(1)}, u32[]{:S(2)}, u32[]{:S(2)}) collective-permute-start(f32[4,768,64]{1,2,0:T(8,128)} %get-tuple-element.432), channel_id=1, source_target_pairs={{1,0},{2,1},{3,2},{4,3},{5,4},{6,5},{7,6},{8,7},{9,8},{10,9},{11,1... | collective-permute-start | bytes 2359304 | tf_op jit(solution)/shard_map/ppermute | solution.py:20
  373.1 15.3 %collective-permute-done.6 = f32[4,768,64]{1,2,0:T(8,128)S(1)} collective-permute-done((f32[4,768,64]{1,2,0:T(8,128)S(1)}, f32[4,768,64]{1,2,0:T(8,128)S(1)}, u32[]{:S(2)}, u32[]{:S(2)}) %collective-permute-start.6) | collective-permute-done | bytes 786464 | tf_op jit(solution)/shard_map/ppermute | solution.py:19
  388.6 1.9 collective-permute-done.7
  393.0 1.6 slice_add_fusion.1
  394.6 6.1 %fusion.102 = f32[4,512,512]{2,1,0:T(8,128)} fusion(f32[4,512,512]{2,1,0:T(8,128)} %param.7, f32[4,64,512]{2,1,0:T(8,128)S(1)} %get-tuple-element.446, f32[4,64,512]{2,1,0:T(8,128)S(1)} %get-tuple-element.445, f32[4,512,64]{2,1,0:T(8,128)S(1)} %copy.29, f32[4,512,64]{2,1,0:T(8,128)S(1)} %copy.28, f32[4,640,640]{2,1,0:T(8,128)} %get-tuple-element.337, ...), kind=kLoop, calls=%fused_computation.142 | loop fusion | flops 8388608 | bytes 15732736 | tf_op jit(solution)/shard_map/sub | solution.py:142
  (294 shorter events, 146.4 us)
Async XLA Ops:
  1.3 10.8 %collective-permute-start = (f32[4,64,512]{2,1,0:T(8,128)S(1)}, f32[4,64,512]{2,1,0:T(8,128)S(1)}, u32[]{:S(2)}, u32[]{:S(2)}) collective-permute-start(f32[4,64,512]{2,1,0:T(8,128)S(1)} %get-tuple-element.437), channel_id=1, source_target_pairs={{0,16},{16,32},{32,48},{48,64},{64,80},{80,96},{96,112},{112,128},... | collective-permute-start | bytes 1572872 | tf_op jit(solution)/shard_map/ppermute | solution.py:19
  5.0 10.5 %collective-permute-start.1 = (f32[4,64,512]{2,1,0:T(8,128)S(1)}, f32[4,64,512]{2,1,0:T(8,128)S(1)}, u32[]{:S(2)}, u32[]{:S(2)}) collective-permute-start(f32[4,64,512]{2,1,0:T(8,128)S(1)} %get-tuple-element.438), channel_id=1, source_target_pairs={{16,0},{32,16},{48,32},{64,48},{80,64},{96,80},{112,96},{128,112},... | collective-permute-start | bytes 1572872 | tf_op jit(solution)/shard_map/ppermute | solution.py:20
  18.6 22.3 %collective-permute-start.2 = (f32[4,640,64]{1,2,0:T(8,128)}, f32[4,640,64]{1,2,0:T(8,128)S(1)}, u32[]{:S(2)}, u32[]{:S(2)}) collective-permute-start(f32[4,640,64]{1,2,0:T(8,128)} %get-tuple-element.435), channel_id=1, source_target_pairs={{0,1},{1,2},{2,3},{3,4},{4,5},{5,6},{6,7},{7,8},{8,9},{9,10},{10,1... | collective-permute-start | bytes 1966088 | tf_op jit(solution)/shard_map/ppermute | solution.py:19
  22.1 20.6 %collective-permute-start.3 = (f32[4,640,64]{1,2,0:T(8,128)}, f32[4,640,64]{1,2,0:T(8,128)}, u32[]{:S(2)}, u32[]{:S(2)}) collective-permute-start(f32[4,640,64]{1,2,0:T(8,128)} %get-tuple-element.436), channel_id=1, source_target_pairs={{1,0},{2,1},{3,2},{4,3},{5,4},{6,5},{7,6},{8,7},{9,8},{10,9},{11,1... | collective-permute-start | bytes 1966088 | tf_op jit(solution)/shard_map/ppermute | solution.py:20
  48.6 3.2 copy-start.2
  344.1 12.9 %collective-permute-start.4 = (f32[4,64,640]{2,1,0:T(8,128)S(1)}, f32[4,64,640]{2,1,0:T(8,128)S(1)}, u32[]{:S(2)}, u32[]{:S(2)}) collective-permute-start(f32[4,64,640]{2,1,0:T(8,128)S(1)} %get-tuple-element.433), channel_id=1, source_target_pairs={{0,16},{16,32},{32,48},{48,64},{64,80},{80,96},{96,112},{112,128},... | collective-permute-start | bytes 1966088 | tf_op jit(solution)/shard_map/ppermute | solution.py:19
  347.0 12.0 %collective-permute-start.5 = (f32[4,64,640]{2,1,0:T(8,128)S(1)}, f32[4,64,640]{2,1,0:T(8,128)}, u32[]{:S(2)}, u32[]{:S(2)}) collective-permute-start(f32[4,64,640]{2,1,0:T(8,128)S(1)} %get-tuple-element.434), channel_id=1, source_target_pairs={{16,0},{32,16},{48,32},{64,48},{80,64},{96,80},{112,96},{128,112},... | collective-permute-start | bytes 1966088 | tf_op jit(solution)/shard_map/ppermute | solution.py:20
  357.1 0.8 copy-start
  363.1 29.8 %copy-start.1 = (f32[4,64,640]{2,1,0:T(8,128)S(1)}, f32[4,64,640]{2,1,0:T(8,128)}, u32[]{:S(2)}) copy-start(f32[4,64,640]{2,1,0:T(8,128)} %copy-done) | copy-start | bytes 1966084
  363.2 25.2 %collective-permute-start.6 = (f32[4,768,64]{1,2,0:T(8,128)S(1)}, f32[4,768,64]{1,2,0:T(8,128)S(1)}, u32[]{:S(2)}, u32[]{:S(2)}) collective-permute-start(f32[4,768,64]{1,2,0:T(8,128)S(1)} %get-tuple-element.431), channel_id=1, source_target_pairs={{0,1},{1,2},{2,3},{3,4},{4,5},{5,6},{6,7},{7,8},{8,9},{9,10},{10,1... | collective-permute-start | bytes 2359304 | tf_op jit(solution)/shard_map/ppermute | solution.py:19
  365.2 25.3 %collective-permute-start.7 = (f32[4,768,64]{1,2,0:T(8,128)}, f32[4,768,64]{1,2,0:T(8,128)S(1)}, u32[]{:S(2)}, u32[]{:S(2)}) collective-permute-start(f32[4,768,64]{1,2,0:T(8,128)} %get-tuple-element.432), channel_id=1, source_target_pairs={{1,0},{2,1},{3,2},{4,3},{5,4},{6,5},{7,6},{8,7},{9,8},{10,9},{11,1... | collective-permute-start | bytes 2359304 | tf_op jit(solution)/shard_map/ppermute | solution.py:20
where the time goes:
time: 408 us; the launch traced here: 401 us
  local copies, waits for them, and re-layouts  125 us (31%)
  matrix products  114 us (28%)
  other arithmetic  73.7 us (18%)
  waiting for transfers between devices  32.3 us (8%)
  starting transfers between devices  30.3 us (7%)
  loops' own time  24.9 us (6%)
    dynamic_update_slice x9, local copies, waits for them, and re-layouts, accumulate(): lax.dynamic_update_slice(gradient, current + spread, (zero, top, zero))  73.2 us
    dot_general x54, matrix products, transform(): first = jnp.dot(left, stacked, preferred_element_type=jnp.float32)  46.8 us
    dot_general x54, matrix products, transform(): result = jnp.dot(middle, right, preferred_element_type=jnp.float32)  45.1 us
    another operation x56, other arithmetic  43 us
    another operation x1, loops' own time, per_device(): lax.fori_loop(0, offsets.shape[2], accumulate, jnp.zeros((4, extent, exte...  24.9 us
    ppermute x4, waiting for transfers between devices, padded_2(): before = lax.ppermute(last, axis, up)  24.5 us
    dot_general x9, matrix products, accumulate(): jnp.dot(piece.reshape(4 * width, width), placer, preferred_element_type=j...  22.2 us
    ppermute x4, starting transfers between devices, padded_2(): after = lax.ppermute(initial, axis, down)  18.2 us
  transfers between devices with their start and end apart: 8, of which 6 were waited for; matrix products, arithmetic and copies ran while one was open for 4% of the time, Pallas kernels for 0%

commit v1 on v0

v1 whole, which is shorter than its diff:
```python
import functools

import jax
import jax.numpy as jnp
import numpy as np
from jax import lax
from jax.experimental import pallas as pl
from jax.experimental.pallas import tpu as pltpu
from jax.sharding import PartitionSpec as P

HALO = 64
RATE = 0.5
LANES = 128
HALF = 64
MESH = pl.DeviceIdType.MESH
BF16 = jnp.bfloat16
F32 = jnp.float32
ANY = pl.BlockSpec(memory_space=pl.ANY)


@functools.cache
def tables(width):
    index = np.arange(width)
    angle = 2.0 * np.pi / width * (index[:, None] * index[None, :] % width)
    norm = 1.0 / np.sqrt(width)
    cosine = (np.cos(angle) * norm).astype(np.float32)
    sine = (np.sin(angle) * norm).astype(np.float32)

    def left(r, i):
        return np.concatenate(
            [np.concatenate([r, -i], 1), np.concatenate([i, r], 1)], 0
        ).astype(BF16)

    def right(r, i):
        return np.concatenate(
            [np.concatenate([r, i], 1), np.concatenate([-i, r], 1)], 0
        ).astype(BF16)

    h = width // 2
    split = []
    for parity in (0, 1):
        split.append(left(cosine[parity::2, :h], -sine[parity::2, :h]))
    for parity in (0, 1):
        split.append(left(cosine[:h, parity::2], sine[:h, parity::2]))
    return np.stack(split), np.stack([right(cosine, -sine), right(cosine, sine)])


def lane_index(shape):
    return lax.broadcasted_iota(jnp.int32, shape, len(shape) - 1)


def pack_high(re, im):
    return jnp.where(lane_index(re.shape) < HALF, pltpu.roll(re, HALF, re.ndim - 1), im)


def pack_low(re, im):
    return jnp.where(lane_index(re.shape) < HALF, re, pltpu.roll(im, HALF, im.ndim - 1))


def pack_kernel(left_ref, right_ref, low_ref, high_ref):
    for s in range(2):
        low_ref[s] = pack_low(left_ref[2 * s], left_ref[2 * s + 1])
        high_ref[s] = pack_high(right_ref[2 * s], right_ref[2 * s + 1])


def pack_edges(objects):
    tile = objects.shape[1]
    last = objects.shape[2] // LANES - 1
    return pl.pallas_call(
        pack_kernel,
        grid=(1,),
        out_shape=[jax.ShapeDtypeStruct((2, tile, LANES), F32)] * 2,
        in_specs=[
            pl.BlockSpec((4, tile, LANES), lambda i: (0, 0, 0)),
            pl.BlockSpec((4, tile, LANES), lambda i: (0, 0, last)),
        ],
        out_specs=[pl.BlockSpec((2, tile, LANES), lambda i: (0, 0, 0))] * 2,
    )(objects, objects)


def exchange_kernel(base, first, rows, cols, up_src, down_src, left_src, right_src,
                    from_up, from_down, from_left, from_right, send, recv):
    tile = rows
    me_r, me_c = lax.axis_index("row"), lax.axis_index("col")
    n_r, n_c = lax.axis_size("row"), lax.axis_size("col")
    north, south = lax.rem(me_r + n_r - 1, n_r), lax.rem(me_r + 1, n_r)
    west, east = lax.rem(me_c + n_c - 1, n_c), lax.rem(me_c + 1, n_c)
    others = [(north, me_c), (south, me_c), (me_r, west), (me_r, east),
              (north, west), (north, east), (south, west), (south, east)]
    barrier = pltpu.get_barrier_semaphore()
    for other in others:
        pl.semaphore_signal(barrier, inc=1, device_id=other, device_id_type=MESH)
    pl.semaphore_wait(barrier, len(others))
    up_rows, main_rows, down_rows = pl.ds(0, HALO), pl.ds(HALO, tile), pl.ds(HALO + tile, HALO)
    if first:
        left_main, up_part, down_part = pl.ds(0, tile), pl.ds(0, HALO), pl.ds(tile - HALO, HALO)
        above, below = up_src.at[:, pl.ds(0, HALO), :], down_src.at[:, pl.ds(tile - HALO, HALO), :]
    else:
        left_main, up_part, down_part = main_rows, up_rows, down_rows
        above, below = up_src, down_src
    moves = [
        (left_src.at[:, left_main], from_right.at[:, main_rows], 2),
        (right_src.at[:, left_main], from_left.at[:, main_rows], 3),
        (left_src.at[:, up_part], from_right.at[:, down_rows], 4),
        (right_src.at[:, up_part], from_left.at[:, down_rows], 5),
        (left_src.at[:, down_part], from_right.at[:, up_rows], 6),
        (right_src.at[:, down_part], from_left.at[:, up_rows], 7),
        (above, from_down, 0),
        (below, from_up, 1),
    ]
    copies = []
    for src, dst, k in moves:
        copy = pltpu.make_async_remote_copy(
            src_ref=src, dst_ref=dst, send_sem=send.at[k], recv_sem=recv.at[k],
            device_id=others[k], device_id_type=MESH,
        )
        copy.start()
        copies.append(copy)
    for copy in copies:
        copy.wait()


def exchange(up, down, left, right, tile, first):
    def body(*refs):
        exchange_kernel(0, first, tile, tile, *refs)

    return pl.pallas_call(
        body,
        out_shape=[jax.ShapeDtypeStruct((4, HALO, tile), F32)] * 2
        + [jax.ShapeDtypeStruct((2, tile + 2 * HALO, LANES), F32)] * 2,
        in_specs=[ANY] * 4,
        out_specs=[ANY] * 4,
        scratch_shapes=[pltpu.SemaphoreType.DMA((8,)), pltpu.SemaphoreType.DMA((8,))],
        compiler_params=pltpu.CompilerParams(
            collective_id=0 if first else 1, has_side_effects=True
        ),
        name="halo_in" if first else "halo_out",
    )(up, down, left, right)


def forward(xr, xi, left, right):
    h = xr.shape[0] // 2
    sums = jnp.concatenate([xr[:h] + xr[h:], xi[:h] + xi[h:]], 0).astype(BF16)
    gaps = jnp.concatenate([xr[:h] - xr[h:], xi[:h] - xi[h:]], 0).astype(BF16)
    even = jnp.dot(left[0], sums, preferred_element_type=F32).astype(BF16)
    odd = jnp.dot(left[1], gaps, preferred_element_type=F32).astype(BF16)
    middle = jnp.concatenate(
        [
            jnp.concatenate([even[:h], even[h:]], 1),
            jnp.concatenate([odd[:h], odd[h:]], 1),
        ],
        0,
    )
    out = jnp.dot(middle, right[0], preferred_element_type=F32)
    return out[:, : 2 * h], out[:, 2 * h :]


def inverse(xr, xi, left, right):
    h = xr.shape[0] // 2
    even = jnp.concatenate([xr[:h], xi[:h]], 0).astype(BF16)
    odd = jnp.concatenate([xr[h:], xi[h:]], 0).astype(BF16)
    e = jnp.dot(left[2], even, preferred_element_type=F32)
    o = jnp.dot(left[3], odd, preferred_element_type=F32)
    top, bottom = (e + o).astype(BF16), (e - o).astype(BF16)
    middle = jnp.concatenate(
        [
            jnp.concatenate([top[:h], top[h:]], 1),
            jnp.concatenate([bottom[:h], bottom[h:]], 1),
        ],
        0,
    )
    out = jnp.dot(middle, right[1], preferred_element_type=F32)
    return out[:, : 2 * h], out[:, 2 * h :]


def compute_kernel(
    offsets, objects, up, down, west, east, probe_in, kernel_in, measured_in, left_in, right_in,
    partial, g_up, g_down, g_west, g_east,
    ext, acc, probe, plain, kern, measured, left, right, turned, held, strips, edge, sems,
):
    tile = objects.shape[1]
    width = probe.shape[1]
    h = width // 2
    n_tiles = tile // LANES
    inner = pl.ds(HALO, tile)
    copies = []

    def start(src, dst):
        copy = pltpu.make_async_copy(src, dst, sems.at[len(copies)])
        copy.start()
        copies.append(copy)

    for t in range(n_tiles):
        lanes = pl.ds(t * LANES, LANES)
        start(objects.at[:, :, lanes], ext.at[:, 1 + t, inner, :])
        start(up.at[:, :, lanes], ext.at[:, 1 + t, pl.ds(0, HALO), :])
        start(down.at[:, :, lanes], ext.at[:, 1 + t, pl.ds(HALO + tile, HALO), :])
    start(west, edge.at[0])
    start(east, edge.at[1])
    start(probe_in, probe)
    start(left_in, left)
    start(right_in, right)
    for t in range(width // LANES):
        lanes = pl.ds(t * LANES, LANES)
        start(kernel_in.at[:, :, lanes], plain.at[:, t])
        start(measured_in.at[0, 0, :, :, lanes], measured.at[:, t])
    acc[...] = jnp.zeros_like(acc)
    for copy in copies:
        copy.wait()
    for s in range(2):
        both = edge[0, s]
        ext[2 * s, 0] = pltpu.roll(both, HALF, 1)
        ext[2 * s + 1, 0] = both
        both = edge[1, s]
        ext[2 * s, n_tiles + 1] = both
        ext[2 * s + 1, n_tiles + 1] = pltpu.roll(both, HALF, 1)
    for k in range(2):
        for parity in range(2):
            for t in range(width // LANES):
                kern[k, pl.ds(parity * h, h), pl.ds(t * LANES, LANES)] = plain[
                    k, t, pl.ds(parity, h, stride=2), :
                ]

    def position(p, carry):
        top = offsets[0, 0, p, 0] + HALO
        start_col = offsets[0, 0, p, 1] + LANES
        q = start_col // LANES
        r = start_col - q * LANES
        rows = pl.ds(top, width)
        keep = lane_index((width, LANES)) >= r

        def window(plane):
            first = jnp.where(keep, ext[plane, q, rows, :], ext[plane, q + 2, rows, :])
            return jnp.concatenate([first, ext[plane, q + 1, rows, :]], 1)

        def add(plane, value):
            first = value[:, :LANES]
            acc[plane, q, rows, :] += jnp.where(keep, first, 0.0)
            acc[plane, q + 1, rows, :] += value[:, LANES:]
            acc[plane, q + 2, rows, :] += jnp.where(keep, 0.0, first)

        for k in range(2):
            turned[k] = pltpu.roll(probe[k], r, 1)
        pr, pim = turned[0], turned[1]
        o1r, o1i = window(0), window(1)
        fr, fi = forward(pr * o1r - pim * o1i, pr * o1i + pim * o1r, left, right)
        kr, kim = kern[0], kern[1]
        sr, si = inverse(kr * fr - kim * fi, kr * fi + kim * fr, left, right)
        held[0] = sr
        held[1] = si
        o2r, o2i = window(2), window(3)
        zr, zi = forward(sr * o2r - si * o2i, sr * o2i + si * o2r, left, right)
        amplitude = jnp.concatenate(
            [
                jnp.concatenate(
                    [measured[p, t, pl.ds(k, h, stride=2), :] for t in range(width // LANES)], 1
                )
                for k in range(2)
            ],
            0,
        )
        factor = 1.0 - amplitude * lax.rsqrt(zr * zr + zi * zi + 1.0)
        gr, gi = inverse(zr * factor, zi * factor, left, right)
        sr, si = held[0], held[1]
        add(2, sr * gr + si * gi)
        add(3, sr * gi - si * gr)
        o2r, o2i = window(2), window(3)
        ur, ui = forward(o2r * gr + o2i * gi, o2r * gi - o2i * gr, left, right)
        kr, kim = kern[0], kern[1]
        wr, wi = inverse(kr * ur + kim * ui, kr * ui - kim * ur, left, right)
        pr, pim = turned[0], turned[1]
        add(0, pr * wr + pim * wi)
        add(1, pr * wi - pim * wr)
        return carry

    lax.fori_loop(0, measured.shape[0], position, 0)

    copies = []
    for t in range(n_tiles):
        lanes = pl.ds(t * LANES, LANES)
        start(acc.at[:, 1 + t, pl.ds(0, HALO), :], g_up.at[:, :, lanes])
        start(acc.at[:, 1 + t, pl.ds(HALO + tile, HALO), :], g_down.at[:, :, lanes])
    for s in range(2):
        strips[0, s] = pack_high(acc[2 * s, 0], acc[2 * s + 1, 0])
        strips[1, s] = pack_low(acc[2 * s, n_tiles + 1], acc[2 * s + 1, n_tiles + 1])
    start(strips.at[0], g_west)
    start(strips.at[1], g_east)
    for t in range(n_tiles):
        ext[:, 1 + t, inner, :] = ext[:, 1 + t, inner, :] - RATE * acc[:, 1 + t, inner, :]
        start(ext.at[:, 1 + t, inner, :], partial.at[:, :, pl.ds(t * LANES, LANES)])
    for copy in copies:
        copy.wait()


def compute(objects, halos, probe, kernel, measured, offsets):
    tile, width = objects.shape[1], probe.shape[1]
    n_tiles = tile // LANES
    extent = tile + 2 * HALO
    left, right = tables(width)
    positions = measured.shape[2]
    return pl.pallas_call(
        compute_kernel,
        out_shape=[jax.ShapeDtypeStruct(objects.shape, F32)]
        + [jax.ShapeDtypeStruct((4, HALO, tile), F32)] * 2
        + [jax.ShapeDtypeStruct((2, extent, LANES), F32)] * 2,
        in_specs=[pl.BlockSpec(memory_space=pltpu.SMEM)] + [ANY] * 10,
        out_specs=[ANY] * 5,
        scratch_shapes=[
            pltpu.VMEM((4, n_tiles + 2, extent, LANES), F32),
            pltpu.VMEM((4, n_tiles + 2, extent, LANES), F32),
            pltpu.VMEM(probe.shape, F32),
            pltpu.VMEM((2, width // LANES, width, LANES), F32),
            pltpu.VMEM(probe.shape, F32),
            pltpu.VMEM((positions, width // LANES, width, LANES), F32),
            pltpu.VMEM(left.shape, BF16),
            pltpu.VMEM(right.shape, BF16),
            pltpu.VMEM(probe.shape, F32),
            pltpu.VMEM(probe.shape, F32),
            pltpu.VMEM((2, 2, extent, LANES), F32),
            pltpu.VMEM((2, 2, extent, LANES), F32),
            pltpu.SemaphoreType.DMA((32,)),
        ],
        compiler_params=pltpu.CompilerParams(vmem_limit_bytes=60 * 2**20),
        name="positions",
    )(offsets, objects, *halos, probe, kernel, measured, jnp.asarray(left), jnp.asarray(right))


def border_kernel(partial, up, down, west, east, out, top, bottom, first, last, rows, edge, sems):
    tile = out.shape[1]
    middle = tile - 2 * HALO
    rest = pl.ds(HALO, middle)
    final = pl.ds(out.shape[2] - LANES, LANES)
    copies = []

    def start(src, dst):
        copy = pltpu.make_async_copy(src, dst, sems.at[len(copies)])
        copy.start()
        copies.append(copy)

    targets = [
        (top, out.at[:, pl.ds(0, HALO), :]),
        (bottom, out.at[:, pl.ds(tile - HALO, HALO), :]),
        (first, out.at[:, rest, pl.ds(0, LANES)]),
        (last, out.at[:, rest, final]),
    ]
    for buffer, place in targets:
        start(place, buffer)
    start(up, rows.at[0])
    start(down, rows.at[1])
    start(west, edge.at[0])
    start(east, edge.at[1])
    for copy in copies:
        copy.wait()

    low = lane_index((1, LANES)) < HALF

    def sides(s, begin, count):
        both = edge[0, s, pl.ds(begin, count), :]
        at_first = (jnp.where(low, both, 0.0), jnp.where(low, pltpu.roll(both, HALF, 1), 0.0))
        both = edge[1, s, pl.ds(begin, count), :]
        at_last = (jnp.where(low, 0.0, pltpu.roll(both, HALF, 1)), jnp.where(low, 0.0, both))
        return at_first, at_last

    top[...] = top[...] - RATE * rows[0]
    bottom[...] = bottom[...] - RATE * rows[1]
    for s in range(2):
        at_first, at_last = sides(s, 2 * HALO, middle)
        for k in range(2):
            first[2 * s + k] = first[2 * s + k] - RATE * at_first[k]
            last[2 * s + k] = last[2 * s + k] - RATE * at_last[k]
        for buffer, main, corner in ((top, HALO, 0), (bottom, tile, tile + HALO)):
            mf, ml = sides(s, main, HALO)
            cf, cl = sides(s, corner, HALO)
            for k in range(2):
                p = 2 * s + k
                buffer[p, :, pl.ds(0, LANES)] = buffer[p, :, pl.ds(0, LANES)] - RATE * (mf[k] + cf[k])
                buffer[p, :, final] = buffer[p, :, final] - RATE * (ml[k] + cl[k])
    copies = []
    for buffer, place in targets:
        start(buffer, place)
    for copy in copies:
        copy.wait()


def border(partial, received):
    tile = partial.shape[1]
    extent = tile + 2 * HALO
    return pl.pallas_call(
        border_kernel,
        out_shape=jax.ShapeDtypeStruct(partial.shape, F32),
        in_specs=[ANY] * 5,
        out_specs=ANY,
        scratch_shapes=[
            pltpu.VMEM((4, HALO, tile), F32),
            pltpu.VMEM((4, HALO, tile), F32),
            pltpu.VMEM((4, tile - 2 * HALO, LANES), F32),
            pltpu.VMEM((4, tile - 2 * HALO, LANES), F32),
            pltpu.VMEM((2, 4, HALO, tile), F32),
            pltpu.VMEM((2, 2, extent, LANES), F32),
            pltpu.SemaphoreType.DMA((16,)),
        ],
        input_output_aliases={0: 0},
        name="border",
    )(partial, *received)


def per_device(objects, probe, kernel, measured, offsets):
    tile = objects.shape[1]
    low, high = pack_edges(objects)
    halos = exchange(objects, objects, low, high, tile, True)
    partial, *strips = compute(objects, halos, probe, kernel, measured, offsets)
    received = exchange(*strips, tile, False)
    return border(partial, received)


def solution(mesh):
    return jax.shard_map(
        per_device,
        mesh=mesh,
        in_specs=(
            P(None, "row", "col"),
            P(),
            P(),
            P("row", "col", None, None, None),
            P("row", "col", None, None),
        ),
        out_specs=P(None, "row", "col"),
        check_vma=False,
    )
```

time: 408 us -> 108 us (0.26)
  the two profiles are of different devices: /device:TPU:27 before, /device:TPU:1 now
where the time goes in v1:
time: 108 us
  Pallas kernels  106 us (98%)
  local copies, waits for them, and re-layouts  1.36 us (1%)
    pallas_call x2, Pallas kernels, exchange(): pl.pallas_call(body, out_shape=[jax.ShapeDtypeStruct((4, HALO, tile), F32...  63.1 us
    pallas_call x1, Pallas kernels, compute(): pl.pallas_call(compute_kernel, out_shape=[jax.ShapeDtypeStruct(objects.sh...  36 us
    pallas_call x1, Pallas kernels, border(): pl.pallas_call(border_kernel, out_shape=jax.ShapeDtypeStruct(partial.shap...  4.43 us
    pallas_call x1, Pallas kernels, pack_edges(): pl.pallas_call(pack_kernel, grid=(1,), out_shape=[jax.ShapeDtypeStruct((2...  2.81 us

profile of v1, /device:TPU:1, one launch (start us, length us, event | category | flops | bytes accessed | tf_op | source)
XLA Modules:
  0.0 107.7 jit_solution(13154271888506254752)
XLA Ops:
  0.0 1.4 %copy.9.offsets = s32[1,1,9,2]{3,2,1,0:T(8,128)} copy(s32[1,1,9,2]{2,3,1,0:T(2,128)} %param.11) | data formatting | bytes 144 | tf_op args[4]
  1.4 2.8 %shard_map.73 = (f32[2,512,128]{2,1,0:T(8,128)}, f32[2,512,128]{2,1,0:T(8,128)}) custom-call(f32[4,512,512]{2,1,0:T(8,128)} %objects.1, f32[4,512,512]{2,1,0:T(8,128)} %objects.1), custom_call_target="tpu_custom_call" | custom-call | tf_op jit(solution)/shard_map/pallas_call | solution.py:69
  4.2 34.0 %halo_in.1 = (f32[4,64,512]{2,1,0:T(8,128)}, f32[4,64,512]{2,1,0:T(8,128)}, f32[2,640,128]{2,1,0:T(8,128)}, f32[2,640,128]{2,1,0:T(8,128)}) custom-call(f32[4,512,512]{2,1,0:T(8,128)} %objects.1, f32[4,512,512]{2,1,0:T(8,128)} %objects.1, f32[2,512,128]{2,1,0:T(8,128)} %get-tuple-element.20.refs_2_, f32[2,512,128]{2,1,0:T(8,128)} %get-tuple-element.21.refs_3_), custom_call_target="tpu_custom_call" | custom-call | tf_op jit(solution)/shard_map/halo_in/pallas_call | solution.py:127
  38.2 36.0 %positions.1 = (f32[4,512,512]{2,1,0:T(8,128)}, f32[4,64,512]{2,1,0:T(8,128)}, f32[4,64,512]{2,1,0:T(8,128)}, f32[2,640,128]{2,1,0:T(8,128)}, f32[2,640,128]{2,1,0:T(8,128)}) custom-call(s32[1,1,9,2]{3,2,1,0:T(8,128)} %copy.9.offsets, f32[4,512,512]{2,1,0:T(8,128)} %objects.1, f32[4,64,512]{2,1,0:T(8,128)} %get-tuple-element.22.up, ...), custom_call_target="tpu_custom_call" | custom-call | tf_op jit(solution)/shard_map/positions/pallas_call | solution.py:301
  74.2 29.1 %halo_out.1 = (f32[4,64,512]{2,1,0:T(8,128)}, f32[4,64,512]{2,1,0:T(8,128)}, f32[2,640,128]{2,1,0:T(8,128)}, f32[2,640,128]{2,1,0:T(8,128)}) custom-call(f32[4,64,512]{2,1,0:T(8,128)} %get-tuple-element.27.refs_0_, f32[4,64,512]{2,1,0:T(8,128)} %get-tuple-element.28.refs_1_, f32[2,640,128]{2,1,0:T(8,128)} %get-tuple-element.29.refs_2_, ...), custom_call_target="tpu_custom_call" | custom-call | tf_op jit(solution)/shard_map/halo_out/pallas_call | solution.py:127
  103.2 4.4 %border.1 = f32[4,512,512]{2,1,0:T(8,128)} custom-call(f32[4,512,512]{2,1,0:T(8,128)} %get-tuple-element.26.partial, f32[4,64,512]{2,1,0:T(8,128)} %get-tuple-element.31.up, f32[4,64,512]{2,1,0:T(8,128)} %get-tuple-element.32.down, f32[2,640,128]{2,1,0:T(8,128)} %get-tuple-element.33.west, ...), custom_call_target="tpu_custom_call", output_to_operand_aliasing={{}: (0, {})} | custom-call | tf_op jit(solution)/shard_map/border/pallas_call | solution.py:388

commit v2 on v0

v2 whole, which is shorter than its diff:
```python
import functools

import jax
import jax.numpy as jnp
import numpy as np
from jax import lax
from jax.experimental import pallas as pl
from jax.experimental.pallas import tpu as pltpu
from jax.sharding import PartitionSpec as P

HALO = 64
RATE = 0.5
LANES = 128
HALF = 64
MESH = pl.DeviceIdType.MESH
BF16 = jnp.bfloat16
F32 = jnp.float32
ANY = pl.BlockSpec(memory_space=pl.ANY)


@functools.cache
def tables(width):
    index = np.arange(width)
    angle = 2.0 * np.pi / width * (index[:, None] * index[None, :] % width)
    norm = 1.0 / np.sqrt(width)
    cosine = (np.cos(angle) * norm).astype(np.float32)
    sine = (np.sin(angle) * norm).astype(np.float32)

    def left(r, i):
        return np.concatenate(
            [np.concatenate([r, -i], 1), np.concatenate([i, r], 1)], 0
        ).astype(BF16)

    def right(r, i):
        return np.concatenate(
            [np.concatenate([r, i], 1), np.concatenate([-i, r], 1)], 0
        ).astype(BF16)

    h = width // 2
    split = []
    for parity in (0, 1):
        split.append(left(cosine[parity::2, :h], -sine[parity::2, :h]))
    for parity in (0, 1):
        split.append(left(cosine[:h, parity::2], sine[:h, parity::2]))
    return np.stack(split), np.stack([right(cosine, -sine), right(cosine, sine)])


def lane_index(shape):
    return lax.broadcasted_iota(jnp.int32, shape, len(shape) - 1)


def pack_high(re, im):
    return jnp.where(lane_index(re.shape) < HALF, pltpu.roll(re, HALF, re.ndim - 1), im)


def pack_low(re, im):
    return jnp.where(lane_index(re.shape) < HALF, re, pltpu.roll(im, HALF, im.ndim - 1))


def forward(xr, xi, left, right):
    h = xr.shape[0] // 2
    sums = jnp.concatenate([xr[:h] + xr[h:], xi[:h] + xi[h:]], 0).astype(BF16)
    gaps = jnp.concatenate([xr[:h] - xr[h:], xi[:h] - xi[h:]], 0).astype(BF16)
    even = jnp.dot(left[0], sums, preferred_element_type=F32).astype(BF16)
    odd = jnp.dot(left[1], gaps, preferred_element_type=F32).astype(BF16)
    middle = jnp.concatenate(
        [
            jnp.concatenate([even[:h], even[h:]], 1),
            jnp.concatenate([odd[:h], odd[h:]], 1),
        ],
        0,
    )
    out = jnp.dot(middle, right[0], preferred_element_type=F32)
    return out[:, : 2 * h], out[:, 2 * h :]


def inverse(xr, xi, left, right):
    h = xr.shape[0] // 2
    even = jnp.concatenate([xr[:h], xi[:h]], 0).astype(BF16)
    odd = jnp.concatenate([xr[h:], xi[h:]], 0).astype(BF16)
    e = jnp.dot(left[2], even, preferred_element_type=F32)
    o = jnp.dot(left[3], odd, preferred_element_type=F32)
    top, bottom = (e + o).astype(BF16), (e - o).astype(BF16)
    middle = jnp.concatenate(
        [
            jnp.concatenate([top[:h], top[h:]], 1),
            jnp.concatenate([bottom[:h], bottom[h:]], 1),
        ],
        0,
    )
    out = jnp.dot(middle, right[1], preferred_element_type=F32)
    return out[:, : 2 * h], out[:, 2 * h :]


def step_kernel(
    offsets, objects, probe_in, kernel_in, measured_in, left_in, right_in,
    out,
    ext1, ext2, probe, turned, plain, kern, measured, left, right, held, pieces,
    strips, edge1, edge2, g_rows1, g_rows2, g_cols1, g_cols2, r_rows1, r_rows2, r_cols1, r_cols2,
    load_sems, send, recv, out_sems,
):
    tile = objects.shape[1]
    width = probe.shape[1]
    h = width // 2
    n_tiles = tile // LANES
    positions = measured.shape[0]
    extent = tile + 2 * HALO
    gap = extent - width
    inner = pl.ds(HALO, tile)
    up_rows, down_rows = pl.ds(0, HALO), pl.ds(HALO + tile, HALO)
    first_rows, last_rows = pl.ds(HALO, HALO), pl.ds(tile, HALO)
    body_tiles = pl.ds(1, n_tiles)
    ext = (ext1, ext2)
    edge = (edge1, edge2)
    g_rows, g_cols = (g_rows1, g_rows2), (g_cols1, g_cols2)
    r_rows, r_cols = (r_rows1, r_rows2), (r_cols1, r_cols2)

    me_r, me_c = lax.axis_index("row"), lax.axis_index("col")
    n_r, n_c = lax.axis_size("row"), lax.axis_size("col")
    north, south = lax.rem(me_r + n_r - 1, n_r), lax.rem(me_r + 1, n_r)
    west, east = lax.rem(me_c + n_c - 1, n_c), lax.rem(me_c + 1, n_c)
    others = [(north, me_c), (south, me_c), (me_r, west), (me_r, east),
              (north, west), (north, east), (south, west), (south, east)]
    barrier = pltpu.get_barrier_semaphore()
    for other in others:
        pl.semaphore_signal(barrier, inc=1, device_id=other, device_id_type=MESH)

    loads = []

    def load(src, dst):
        copy = pltpu.make_async_copy(src, dst, load_sems.at[len(loads)])
        copy.start()
        loads.append(copy)

    for s in range(2):
        for t in range(n_tiles):
            load(objects.at[pl.ds(2 * s, 2), :, pl.ds(t * LANES, LANES)], ext[s].at[:, 1 + t, inner, :])
    n_object = len(loads)
    load(probe_in, probe)
    for t in range(width // LANES):
        load(kernel_in.at[:, :, pl.ds(t * LANES, LANES)], plain.at[:, t])
    load(left_in, left)
    load(right_in, right)
    for t in range(width // LANES):
        load(measured_in.at[0, 0, :, :, pl.ds(t * LANES, LANES)], measured.at[:, t])

    def exchange(phase, above, below, to_west, to_east, base, from_up, from_down, from_west, from_east):
        main = pl.ds(base, tile)
        upper = pl.ds(0, HALO)
        lower = pl.ds(base + tile + base - HALO, HALO)
        landed = inner
        moves = [
            (to_west.at[main], from_east.at[landed], 2),
            (to_east.at[main], from_west.at[landed], 3),
            (to_west.at[upper], from_east.at[down_rows], 4),
            (to_east.at[upper], from_west.at[down_rows], 5),
            (to_west.at[lower], from_east.at[up_rows], 6),
            (to_east.at[lower], from_west.at[up_rows], 7),
            (above, from_down, 0),
            (below, from_up, 1),
        ]
        copies = []
        for src, dst, k in moves:
            copy = pltpu.make_async_remote_copy(
                src_ref=src, dst_ref=dst, send_sem=send.at[phase, k], recv_sem=recv.at[phase, k],
                device_id=others[k], device_id_type=MESH,
            )
            copy.start()
            copies.append(copy)
        return copies

    def send_halo(s):
        e = ext[s]
        return exchange(
            s,
            e.at[:, body_tiles, first_rows, :], e.at[:, body_tiles, last_rows, :],
            strips.at[s, 0], strips.at[s, 1], 0,
            e.at[:, body_tiles, up_rows, :], e.at[:, body_tiles, down_rows, :],
            edge[s].at[0], edge[s].at[1],
        )

    def send_gradient(s):
        g, r = g_rows[s], r_rows[s]
        c, d = g_cols[s], r_cols[s]
        return exchange(
            2 + s, g.at[0], g.at[1], c.at[0], c.at[1], HALO, r.at[0], r.at[1], d.at[0], d.at[1]
        )

    for copy in loads[:n_object]:
        copy.wait()
    for s in range(2):
        strips[s, 0] = pack_low(ext[s][0, 1, inner, :], ext[s][1, 1, inner, :])
        strips[s, 1] = pack_high(ext[s][0, n_tiles, inner, :], ext[s][1, n_tiles, inner, :])
    pl.semaphore_wait(barrier, len(others))
    halo1 = send_halo(0)

    for copy in loads[n_object:]:
        copy.wait()
    pieces[...] = jnp.zeros_like(pieces)
    for k in range(2):
        for parity in range(2):
            for t in range(width // LANES):
                kern[k, pl.ds(parity * h, h), pl.ds(t * LANES, LANES)] = plain[
                    k, t, pl.ds(parity, h, stride=2), :
                ]

    def where_of(p):
        top = offsets[0, 0, p, 0] + HALO
        start = offsets[0, 0, p, 1] + LANES
        q = start // LANES
        return top, start, q, start - q * LANES

    def turn(p, carry):
        r = where_of(p)[3]
        for k in range(2):
            turned[p, k] = pltpu.roll(probe[k], r, 1)
        return carry

    lax.fori_loop(0, positions, turn, 0)

    def unpack_halo(s):
        both = edge[s][0]
        ext[s][0, 0] = pltpu.roll(both, HALF, 1)
        ext[s][1, 0] = both
        both = edge[s][1]
        ext[s][0, n_tiles + 1] = both
        ext[s][1, n_tiles + 1] = pltpu.roll(both, HALF, 1)

    def window(s, plane, p):
        top, _, q, r = where_of(p)
        rows = pl.ds(top, width)
        keep = lane_index((width, LANES)) >= r
        first = jnp.where(keep, ext[s][plane, q, rows, :], ext[s][plane, q + 2, rows, :])
        return jnp.concatenate([first, ext[s][plane, q + 1, rows, :]], 1)

    def put(p, c, value):
        rows = pl.ds(gap + p * extent, width)
        pieces[c, 0, rows, :] = value[:, :LANES]
        pieces[c, 1, rows, :] = value[:, LANES:]

    for copy in halo1:
        copy.wait()
    halo2 = send_halo(1)
    unpack_halo(0)

    def stage_a(p, carry):
        pr, pim = turned[p, 0], turned[p, 1]
        o1r, o1i = window(0, 0, p), window(0, 1, p)
        fr, fi = forward(pr * o1r - pim * o1i, pr * o1i + pim * o1r, left, right)
        kr, kim = kern[0], kern[1]
        sr, si = inverse(kr * fr - kim * fi, kr * fi + kim * fr, left, right)
        held[p, 0] = sr
        held[p, 1] = si
        return carry

    lax.fori_loop(0, positions, stage_a, 0)

    for copy in halo2:
        copy.wait()
    unpack_halo(1)

    def stage_b(p, carry):
        sr, si = held[p, 0], held[p, 1]
        o2r, o2i = window(1, 0, p), window(1, 1, p)
        zr, zi = forward(sr * o2r - si * o2i, sr * o2i + si * o2r, left, right)
        amplitude = jnp.concatenate(
            [
                jnp.concatenate(
                    [measured[p, t, pl.ds(k, h, stride=2), :] for t in range(width // LANES)], 1
                )
                for k in range(2)
            ],
            0,
        )
        factor = 1.0 - amplitude * lax.rsqrt(zr * zr + zi * zi + 1.0)
        gr, gi = inverse(zr * factor, zi * factor, left, right)
        sr, si = held[p, 0], held[p, 1]
        put(p, 0, sr * gr + si * gi)
        put(p, 1, sr * gi - si * gr)
        o2r, o2i = window(1, 0, p), window(1, 1, p)
        held[p, 0] = o2r * gr + o2i * gi
        held[p, 1] = o2r * gi - o2i * gr
        return carry

    lax.fori_loop(0, positions, stage_b, 0)

    def gather(c, t, row, count):
        total = jnp.zeros((count, LANES), F32)
        lane = lane_index((count, LANES)) + t * LANES
        for p in range(positions):
            top, start, q, _ = where_of(p)
            value = pieces[c, (t + 8 - q) % 2, pl.ds(gap + p * extent - top + row, count), :]
            total = total + jnp.where((lane >= start) & (lane < start + width), value, 0.0)
        return total

    def gather_borders(s):
        def sides(i, carry):
            row = pl.multiple_of(i * HALO, HALO)
            rows = pl.ds(row, HALO)
            g_cols[s][0, rows, :] = pack_high(gather(0, 0, row, HALO), gather(1, 0, row, HALO))
            g_cols[s][1, rows, :] = pack_low(
                gather(0, n_tiles + 1, row, HALO), gather(1, n_tiles + 1, row, HALO)
            )
            return carry

        lax.fori_loop(0, extent // HALO, sides, 0)

        def ends(i, carry):
            for c in range(2):
                g_rows[s][0, c, i] = gather(c, 1 + i, 0, HALO)
                g_rows[s][1, c, i] = gather(c, 1 + i, HALO + tile, HALO)
            return carry

        lax.fori_loop(0, n_tiles, ends, 0)

    def gather_inner(s):
        def chunk(i, carry):
            row = pl.multiple_of(HALO + i * HALO, HALO)
            rows = pl.ds(row, HALO)
            for c in range(2):
                for t in range(1, n_tiles + 1):
                    ext[s][c, t, rows, :] = ext[s][c, t, rows, :] - RATE * gather(c, t, row, HALO)
            return carry

        lax.fori_loop(0, tile // HALO, chunk, 0)

    def add_borders(s):
        e = ext[s]
        for t in range(n_tiles):
            for c in range(2):
                e[c, 1 + t, first_rows, :] = e[c, 1 + t, first_rows, :] - RATE * r_rows[s][0, c, t]
                e[c, 1 + t, last_rows, :] = e[c, 1 + t, last_rows, :] - RATE * r_rows[s][1, c, t]
        for rows, source in ((inner, inner), (first_rows, up_rows), (last_rows, down_rows)):
            both = r_cols[s][0, source, :]
            low = lane_index(both.shape) < HALF
            swapped = pltpu.roll(both, HALF, 1)
            e[0, 1, rows, :] = e[0, 1, rows, :] - RATE * jnp.where(low, both, 0.0)
            e[1, 1, rows, :] = e[1, 1, rows, :] - RATE * jnp.where(low, swapped, 0.0)
            both = r_cols[s][1, source, :]
            swapped = pltpu.roll(both, HALF, 1)
            e[0, n_tiles, rows, :] = e[0, n_tiles, rows, :] - RATE * jnp.where(low, 0.0, swapped)
            e[1, n_tiles, rows, :] = e[1, n_tiles, rows, :] - RATE * jnp.where(low, 0.0, both)

    def store(s):
        copies = []
        for t in range(n_tiles):
            copy = pltpu.make_async_copy(
                ext[s].at[:, 1 + t, inner, :],
                out.at[pl.ds(2 * s, 2), :, pl.ds(t * LANES, LANES)],
                out_sems.at[s, t],
            )
            copy.start()
            copies.append(copy)
        return copies

    gather_borders(1)
    sent2 = send_gradient(1)
    gather_inner(1)

    def stage_c(p, carry):
        ur, ui = forward(held[p, 0], held[p, 1], left, right)
        kr, kim = kern[0], kern[1]
        wr, wi = inverse(kr * ur + kim * ui, kr * ui - kim * ur, left, right)
        pr, pim = turned[p, 0], turned[p, 1]
        put(p, 0, pr * wr + pim * wi)
        put(p, 1, pr * wi - pim * wr)
        return carry

    lax.fori_loop(0, positions, stage_c, 0)

    gather_borders(0)
    for copy in sent2:
        copy.wait()
    sent1 = send_gradient(0)
    gather_inner(0)
    add_borders(1)
    stored = store(1)
    for copy in sent1:
        copy.wait()
    add_borders(0)
    stored = stored + store(0)
    for copy in stored:
        copy.wait()


def per_device(objects, probe, kernel, measured, offsets):
    tile, width = objects.shape[1], probe.shape[1]
    n_tiles = tile // LANES
    extent = tile + 2 * HALO
    left, right = tables(width)
    positions = measured.shape[2]
    ext = pltpu.VMEM((2, n_tiles + 2, extent, LANES), F32)
    planes = pltpu.VMEM((positions, 2, width, width), F32)
    cols = pltpu.VMEM((2, extent, LANES), F32)
    rows = pltpu.VMEM((2, 2, n_tiles, HALO, LANES), F32)
    dma = pltpu.SemaphoreType.DMA
    return pl.pallas_call(
        step_kernel,
        out_shape=jax.ShapeDtypeStruct(objects.shape, F32),
        in_specs=[pl.BlockSpec(memory_space=pltpu.SMEM)] + [ANY] * 6,
        out_specs=ANY,
        scratch_shapes=[
            ext,
            ext,
            pltpu.VMEM(probe.shape, F32),
            planes,
            pltpu.VMEM((2, width // LANES, width, LANES), F32),
            pltpu.VMEM(probe.shape, F32),
            pltpu.VMEM((positions, width // LANES, width, LANES), F32),
            pltpu.VMEM(left.shape, BF16),
            pltpu.VMEM(right.shape, BF16),
            planes,
            pltpu.VMEM((2, 2, positions * extent + extent - width, LANES), F32),
            pltpu.VMEM((2, 2, tile, LANES), F32),
            cols, cols, rows, rows, cols, cols, rows, rows, cols, cols,
            dma((24,)), dma((4, 8)), dma((4, 8)), dma((2, n_tiles)),
        ],
        compiler_params=pltpu.CompilerParams(
            vmem_limit_bytes=63 * 2**20, collective_id=0, has_side_effects=True
        ),
        name="step",
    )(offsets, objects, probe, kernel, measured, jnp.asarray(left), jnp.asarray(right))


def solution(mesh):
    return jax.shard_map(
        per_device,
        mesh=mesh,
        in_specs=(
            P(None, "row", "col"),
            P(),
            P(),
            P("row", "col", None, None, None),
            P("row", "col", None, None),
        ),
        out_specs=P(None, "row", "col"),
        check_vma=False,
    )
```

time: 408 us -> 90.5 us (0.22)
  the two profiles are of different devices: /device:TPU:27 before, /device:TPU:8 now
where the time goes in v2:
time: 90.5 us; the launch traced here: 90.4 us
  Pallas kernels  84.4 us (93%)
  local copies, waits for them, and re-layouts  6 us (7%)
    pallas_call x1, Pallas kernels, per_device(): pl.pallas_call(step_kernel, out_shape=jax.ShapeDtypeStruct(objects.shape,...  84.4 us
    unnamed x2, local copies, waits for them, and re-layouts  6 us

profile of v2, /device:TPU:8, one launch (start us, length us, event | category | flops | bytes accessed | tf_op | source)
XLA Modules:
  0.0 90.4 jit_solution(15205918345122391241)
XLA Ops:
  0.0 1.4 %copy.8.offsets = s32[1,1,9,2]{3,2,1,0:T(8,128)} copy(s32[1,1,9,2]{2,3,1,0:T(2,128)} %param.11) | data formatting | bytes 144 | tf_op args[4]
  1.4 84.4 %step.1 = f32[4,512,512]{2,1,0:T(8,128)} custom-call(s32[1,1,9,2]{3,2,1,0:T(8,128)} %copy.8.offsets, f32[4,512,512]{2,1,0:T(8,128)} %objects.1, f32[2,256,256]{2,1,0:T(8,128)} %probe_in.1, f32[2,256,256]{2,1,0:T(8,128)} %kernel_in.1, f32[1,1,9,256,256]{4,3,2,1,0:T(8,128)} %measured_in.1, bf16[4,256,256]{2,1,0:T(8,128)(2,1)} %constant.4.clone.left_in, ...), custom_call_target="tpu_custom_call" | custom-call | tf_op jit(solution)/shard_map/step/pallas_call | solution.py:397
  85.8 4.6 %copy.10 = f32[4,512,512]{2,1,0:T(8,128)} copy(f32[4,512,512]{2,1,0:T(8,128)} %step.1) | data formatting | bytes 8388608

commit v3 on v2

--- a/solution.py
+++ b/solution.py
@@ -97,7 +97,7 @@
     out,
     ext1, ext2, probe, turned, plain, kern, measured, left, right, held, pieces,
     strips, edge1, edge2, g_rows1, g_rows2, g_cols1, g_cols2, r_rows1, r_rows2, r_cols1, r_cols2,
-    load_sems, send, recv, out_sems,
+    load_sems, send, recv,
 ):
     tile = objects.shape[1]
     width = probe.shape[1]
@@ -119,11 +119,21 @@
     n_r, n_c = lax.axis_size("row"), lax.axis_size("col")
     north, south = lax.rem(me_r + n_r - 1, n_r), lax.rem(me_r + 1, n_r)
     west, east = lax.rem(me_c + n_c - 1, n_c), lax.rem(me_c + 1, n_c)
+    has_n, has_s, has_w, has_e = me_r > 0, me_r < n_r - 1, me_c > 0, me_c < n_c - 1
     others = [(north, me_c), (south, me_c), (me_r, west), (me_r, east),
               (north, west), (north, east), (south, west), (south, east)]
+    here = [has_n, has_s, has_w, has_e, has_n & has_w, has_n & has_e, has_s & has_w, has_s & has_e]
+    opposite = [1, 0, 3, 2, 7, 6, 5, 4]
+    for ref in (r_rows1, r_rows2, r_cols1, r_cols2):
+        ref[...] = jnp.zeros_like(ref)
     barrier = pltpu.get_barrier_semaphore()
-    for other in others:
-        pl.semaphore_signal(barrier, inc=1, device_id=other, device_id_type=MESH)
+    neighbours = 0
+    for other, there in zip(others, here):
+        neighbours = neighbours + there.astype(jnp.int32)
+
+        @pl.when(there)
+        def _():
+            pl.semaphore_signal(barrier, inc=1, device_id=other, device_id_type=MESH)
 
     loads = []
 
@@ -135,7 +145,6 @@
     for s in range(2):
         for t in range(n_tiles):
             load(objects.at[pl.ds(2 * s, 2), :, pl.ds(t * LANES, LANES)], ext[s].at[:, 1 + t, inner, :])
-    n_object = len(loads)
     load(probe_in, probe)
     for t in range(width // LANES):
         load(kernel_in.at[:, :, pl.ds(t * LANES, LANES)], plain.at[:, t])
@@ -165,9 +174,14 @@
                 src_ref=src, dst_ref=dst, send_sem=send.at[phase, k], recv_sem=recv.at[phase, k],
                 device_id=others[k], device_id_type=MESH,
             )
-            copy.start()
-            copies.append(copy)
+            pl.when(here[k])(copy.start)
+            copies.append((copy, k))
         return copies
+
+    def finish(copies):
+        for copy, k in copies:
+            pl.when(here[k])(copy.wait_send)
+            pl.when(here[opposite[k]])(copy.wait_recv)
 
     def send_halo(s):
         e = ext[s]
@@ -186,17 +200,25 @@
             2 + s, g.at[0], g.at[1], c.at[0], c.at[1], HALO, r.at[0], r.at[1], d.at[0], d.at[1]
         )
 
-    for copy in loads[:n_object]:
+    for copy in loads[:n_tiles]:
         copy.wait()
-    for s in range(2):
+
+    def pack(s):
         strips[s, 0] = pack_low(ext[s][0, 1, inner, :], ext[s][1, 1, inner, :])
         strips[s, 1] = pack_high(ext[s][0, n_tiles, inner, :], ext[s][1, n_tiles, inner, :])
-    pl.semaphore_wait(barrier, len(others))
+    pack(0)
+    pl.semaphore_wait(barrier, neighbours)
     halo1 = send_halo(0)
 
-    for copy in loads[n_object:]:
+    for copy in loads[n_tiles:]:
         copy.wait()
-    pieces[...] = jnp.zeros_like(pieces)
+    pack(1)
+    def clear(i, carry):
+        rows = pl.ds(pl.multiple_of(i * extent, LANES), gap)
+        pieces[:, :, rows, :] = jnp.zeros((2, 3, gap, LANES), F32)
+        return carry
+
+    lax.fori_loop(0, positions + 1, clear, 0)
     for k in range(2):
         for parity in range(2):
             for t in range(width // LANES):
@@ -205,13 +227,13 @@
                 ]
 
     def where_of(p):
-        top = offsets[0, 0, p, 0] + HALO
-        start = offsets[0, 0, p, 1] + LANES
+        top = offsets[0, 0, 0, p] + HALO
+        start = offsets[0, 0, 1, p] + LANES
         q = start // LANES
-        return top, start, q, start - q * LANES
+        return top, q, start - q * LANES
 
     def turn(p, carry):
-        r = where_of(p)[3]
+        r = where_of(p)[2]
         for k in range(2):
             turned[p, k] = pltpu.roll(probe[k], r, 1)
         return carry
@@ -227,7 +249,7 @@
         ext[s][1, n_tiles + 1] = pltpu.roll(both, HALF, 1)
 
     def window(s, plane, p):
-        top, _, q, r = where_of(p)
+        top, q, r = where_of(p)
         rows = pl.ds(top, width)
         keep = lane_index((width, LANES)) >= r
         first = jnp.where(keep, ext[s][plane, q, rows, :], ext[s][plane, q + 2, rows, :])
@@ -235,11 +257,13 @@
 
     def put(p, c, value):
         rows = pl.ds(gap + p * extent, width)
-        pieces[c, 0, rows, :] = value[:, :LANES]
+        keep = lane_index((width, LANES)) >= where_of(p)[2]
+        first = value[:, :LANES]
+        pieces[c, 0, rows, :] = jnp.where(keep, first, 0.0)
         pieces[c, 1, rows, :] = value[:, LANES:]
-
-    for copy in halo1:
-        copy.wait()
+        pieces[c, 2, rows, :] = jnp.where(keep, 0.0, first)
+
+    finish(halo1)
     halo2 = send_halo(1)
     unpack_halo(0)
 
@@ -253,10 +277,9 @@
         held[p, 1] = si
         return carry
 
-    lax.fori_loop(0, positions, stage_a, 0)
-
-    for copy in halo2:
-        copy.wait()
+    lax.fori_loop(0, positions, stage_a, 0, unroll=3)
+
+    finish(halo2)
     unpack_halo(1)
 
     def stage_b(p, carry):
@@ -282,77 +305,70 @@
         held[p, 1] = o2r * gi - o2i * gr
         return carry
 
-    lax.fori_loop(0, positions, stage_b, 0)
-
-    def gather(c, t, row, count):
-        total = jnp.zeros((count, LANES), F32)
-        lane = lane_index((count, LANES)) + t * LANES
+    lax.fori_loop(0, positions, stage_b, 0, unroll=3)
+
+    def gather(t, row, count):
+        totals = [jnp.zeros((count, LANES), F32)] * 2
         for p in range(positions):
-            top, start, q, _ = where_of(p)
-            value = pieces[c, (t + 8 - q) % 2, pl.ds(gap + p * extent - top + row, count), :]
-            total = total + jnp.where((lane >= start) & (lane < start + width), value, 0.0)
-        return total
+            top, q, _ = spots[p]
+            inside = (t >= q) & (t <= q + 2)
+            slot = jnp.where(inside, t - q, 0)
+            rows = pl.ds(jnp.where(inside, gap + p * extent - top + row, 0), count)
+            totals = [totals[c] + pieces[c, slot, rows, :] for c in range(2)]
+        return totals
 
     def gather_borders(s):
         def sides(i, carry):
             row = pl.multiple_of(i * HALO, HALO)
             rows = pl.ds(row, HALO)
-            g_cols[s][0, rows, :] = pack_high(gather(0, 0, row, HALO), gather(1, 0, row, HALO))
-            g_cols[s][1, rows, :] = pack_low(
-                gather(0, n_tiles + 1, row, HALO), gather(1, n_tiles + 1, row, HALO)
-            )
+            g_cols[s][0, rows, :] = pack_high(*gather(0, row, HALO))
+            g_cols[s][1, rows, :] = pack_low(*gather(n_tiles + 1, row, HALO))
             return carry
 
         lax.fori_loop(0, extent // HALO, sides, 0)
 
         def ends(i, carry):
-            for c in range(2):
-                g_rows[s][0, c, i] = gather(c, 1 + i, 0, HALO)
-                g_rows[s][1, c, i] = gather(c, 1 + i, HALO + tile, HALO)
+            for k in range(2):
+                totals = gather(1 + i, k * (HALO + tile), HALO)
+                for c in range(2):
+                    g_rows[s][k, c, i] = totals[c]
             return carry
 
         lax.fori_loop(0, n_tiles, ends, 0)
 
     def gather_inner(s):
         def chunk(i, carry):
-            row = pl.multiple_of(HALO + i * HALO, HALO)
-            rows = pl.ds(row, HALO)
-            for c in range(2):
-                for t in range(1, n_tiles + 1):
-                    ext[s][c, t, rows, :] = ext[s][c, t, rows, :] - RATE * gather(c, t, row, HALO)
+            row = pl.multiple_of(i * HALO, HALO)
+            for t in range(n_tiles):
+                totals = gather(t + 1, row + HALO, HALO)
+                for c in range(2):
+                    out[2 * s + c, pl.ds(row, HALO), pl.ds(t * LANES, LANES)] = (
+                        ext[s][c, t + 1, pl.ds(row + HALO, HALO), :] - RATE * totals[c]
+                    )
             return carry
 
         lax.fori_loop(0, tile // HALO, chunk, 0)
 
+    def subtract(plane, rows, t, value):
+        lanes = pl.ds(t * LANES, LANES)
+        out[plane, rows, lanes] = out[plane, rows, lanes] - RATE * value
+
     def add_borders(s):
-        e = ext[s]
+        begin, end = pl.ds(0, HALO), pl.ds(tile - HALO, HALO)
         for t in range(n_tiles):
             for c in range(2):
-                e[c, 1 + t, first_rows, :] = e[c, 1 + t, first_rows, :] - RATE * r_rows[s][0, c, t]
-                e[c, 1 + t, last_rows, :] = e[c, 1 + t, last_rows, :] - RATE * r_rows[s][1, c, t]
-        for rows, source in ((inner, inner), (first_rows, up_rows), (last_rows, down_rows)):
+                subtract(2 * s + c, begin, t, r_rows[s][0, c, t])
+                subtract(2 * s + c, end, t, r_rows[s][1, c, t])
+        for rows, source in ((pl.ds(0, tile), inner), (begin, up_rows), (end, down_rows)):
             both = r_cols[s][0, source, :]
             low = lane_index(both.shape) < HALF
-            swapped = pltpu.roll(both, HALF, 1)
-            e[0, 1, rows, :] = e[0, 1, rows, :] - RATE * jnp.where(low, both, 0.0)
-            e[1, 1, rows, :] = e[1, 1, rows, :] - RATE * jnp.where(low, swapped, 0.0)
+            subtract(2 * s, rows, 0, jnp.where(low, both, 0.0))
+            subtract(2 * s + 1, rows, 0, jnp.where(low, pltpu.roll(both, HALF, 1), 0.0))
             both = r_cols[s][1, source, :]
-            swapped = pltpu.roll(both, HALF, 1)
-            e[0, n_tiles, rows, :] = e[0, n_tiles, rows, :] - RATE * jnp.where(low, 0.0, swapped)
-            e[1, n_tiles, rows, :] = e[1, n_tiles, rows, :] - RATE * jnp.where(low, 0.0, both)
-
-    def store(s):
-        copies = []
-        for t in range(n_tiles):
-            copy = pltpu.make_async_copy(
-                ext[s].at[:, 1 + t, inner, :],
-                out.at[pl.ds(2 * s, 2), :, pl.ds(t * LANES, LANES)],
-                out_sems.at[s, t],
-            )
-            copy.start()
-            copies.append(copy)
-        return copies
-
+            subtract(2 * s, rows, n_tiles - 1, jnp.where(low, 0.0, pltpu.roll(both, HALF, 1)))
+            subtract(2 * s + 1, rows, n_tiles - 1, jnp.where(low, 0.0, both))
+
+    spots = [where_of(p) for p in range(positions)]
     gather_borders(1)
     sent2 = send_gradient(1)
     gather_inner(1)
@@ -366,21 +382,15 @@
         put(p, 1, pr * wi - pim * wr)
         return carry
 
-    lax.fori_loop(0, positions, stage_c, 0)
+    lax.fori_loop(0, positions, stage_c, 0, unroll=3)
 
     gather_borders(0)
-    for copy in sent2:
-        copy.wait()
+    finish(sent2)
     sent1 = send_gradient(0)
     gather_inner(0)
     add_borders(1)
-    stored = store(1)
-    for copy in sent1:
-        copy.wait()
+    finish(sent1)
     add_borders(0)
-    stored = stored + store(0)
-    for copy in stored:
-        copy.wait()
 
 
 def per_device(objects, probe, kernel, measured, offsets):
@@ -396,9 +406,9 @@
     dma = pltpu.SemaphoreType.DMA
     return pl.pallas_call(
         step_kernel,
-        out_shape=jax.ShapeDtypeStruct(objects.shape, F32),
+        out_shape=pltpu.VMEM(objects.shape, F32),
         in_specs=[pl.BlockSpec(memory_space=pltpu.SMEM)] + [ANY] * 6,
-        out_specs=ANY,
+        out_specs=pl.BlockSpec(memory_space=pltpu.VMEM),
         scratch_shapes=[
             ext,
             ext,
@@ -410,16 +420,16 @@
             pltpu.VMEM(left.shape, BF16),
             pltpu.VMEM(right.shape, BF16),
             planes,
-            pltpu.VMEM((2, 2, positions * extent + extent - width, LANES), F32),
+            pltpu.VMEM((2, 3, positions * extent + extent - width, LANES), F32),
             pltpu.VMEM((2, 2, tile, LANES), F32),
             cols, cols, rows, rows, cols, cols, rows, rows, cols, cols,
-            dma((24,)), dma((4, 8)), dma((4, 8)), dma((2, n_tiles)),
+            dma((24,)), dma((4, 8)), dma((4, 8)),
         ],
         compiler_params=pltpu.CompilerParams(
-            vmem_limit_bytes=63 * 2**20, collective_id=0, has_side_effects=True
+            vmem_limit_bytes=58 * 2**20, collective_id=0, has_side_effects=True
         ),
         name="step",
-    )(offsets, objects, probe, kernel, measured, jnp.asarray(left), jnp.asarray(right))
+    )(jnp.swapaxes(offsets, 2, 3), objects, probe, kernel, measured, jnp.asarray(left), jnp.asarray(right))
 
 
 def solution(mesh):

time: 90.5 us -> 66.9 us (0.74)
  the two profiles are of different devices: /device:TPU:8 before, /device:TPU:31 now
where the time goes in v3:
time: 66.9 us; the launch traced here: 66.4 us
  Pallas kernels  64.4 us (96%)
  local copies, waits for them, and re-layouts  2.02 us (3%)
    pallas_call x1, Pallas kernels, per_device(): pl.pallas_call(step_kernel, out_shape=pltpu.VMEM(objects.shape, F32), in_...  64.4 us
    unnamed x1, local copies, waits for them, and re-layouts  2.02 us

profile of v3, /device:TPU:31, one launch (start us, length us, event | category | flops | bytes accessed | tf_op | source)
XLA Modules:
  0.0 66.4 jit_solution(1987643485807686765)
XLA Ops:
  0.0 64.4 %step.1 = f32[4,512,512]{2,1,0:T(8,128)S(1)} custom-call(s32[1,1,2,9]{3,2,1,0:T(2,128)} %bitcast.1, f32[4,512,512]{2,1,0:T(8,128)} %objects.1, f32[2,256,256]{2,1,0:T(8,128)} %probe_in.1, f32[2,256,256]{2,1,0:T(8,128)} %kernel_in.1, f32[1,1,9,256,256]{4,3,2,1,0:T(8,128)} %measured_in.1, bf16[4,256,256]{2,1,0:T(8,128)(2,1)} %constant.4.clone.left_in, ...), custom_call_target="tpu_custom_call" | custom-call | tf_op jit(solution)/shard_map/step/pallas_call | solution.py:407
  64.4 2.0 %copy.9 = f32[4,512,512]{2,1,0:T(8,128)} copy(f32[4,512,512]{2,1,0:T(8,128)S(1)} %step.1) | data formatting | bytes 8388608

commit v4 on v3

--- a/solution.py
+++ b/solution.py
@@ -42,7 +42,9 @@
         split.append(left(cosine[parity::2, :h], -sine[parity::2, :h]))
     for parity in (0, 1):
         split.append(left(cosine[:h, parity::2], sine[:h, parity::2]))
-    return np.stack(split), np.stack([right(cosine, -sine), right(cosine, sine)])
+    columns = [right(cosine[:h, k::2], -sine[:h, k::2]) for k in (0, 1)]
+    columns += [right(cosine[k::2, :h], sine[k::2, :h]) for k in (0, 1)]
+    return np.stack(split), np.stack(columns)
 
 
 def lane_index(shape):
@@ -57,45 +59,50 @@
     return jnp.where(lane_index(re.shape) < HALF, re, pltpu.roll(im, HALF, im.ndim - 1))
 
 
+def dot(a, b):
+    return jnp.dot(a, b, preferred_element_type=F32)
+
+
+def join(parts, axis):
+    return jnp.concatenate(parts, axis)
+
+
 def forward(xr, xi, left, right):
     h = xr.shape[0] // 2
-    sums = jnp.concatenate([xr[:h] + xr[h:], xi[:h] + xi[h:]], 0).astype(BF16)
-    gaps = jnp.concatenate([xr[:h] - xr[h:], xi[:h] - xi[h:]], 0).astype(BF16)
-    even = jnp.dot(left[0], sums, preferred_element_type=F32).astype(BF16)
-    odd = jnp.dot(left[1], gaps, preferred_element_type=F32).astype(BF16)
-    middle = jnp.concatenate(
-        [
-            jnp.concatenate([even[:h], even[h:]], 1),
-            jnp.concatenate([odd[:h], odd[h:]], 1),
-        ],
-        0,
-    )
-    out = jnp.dot(middle, right[0], preferred_element_type=F32)
-    return out[:, : 2 * h], out[:, 2 * h :]
+    sums = join([xr[:h] + xr[h:], xi[:h] + xi[h:]], 0).astype(BF16)
+    gaps = join([xr[:h] - xr[h:], xi[:h] - xi[h:]], 0).astype(BF16)
+    even, odd = dot(left[0], sums), dot(left[1], gaps)
+
+    def halves(y, sign):
+        y = y[:, :h] + y[:, h:] if sign > 0 else y[:, :h] - y[:, h:]
+        return join([y[:h], y[h:]], 1).astype(BF16)
+
+    low = dot(join([halves(even, 1), halves(odd, 1)], 0), right[0])
+    high = dot(join([halves(even, -1), halves(odd, -1)], 0), right[1])
+    return join([low[:, :h], high[:, :h]], 1), join([low[:, h:], high[:, h:]], 1)
 
 
 def inverse(xr, xi, left, right):
     h = xr.shape[0] // 2
-    even = jnp.concatenate([xr[:h], xi[:h]], 0).astype(BF16)
-    odd = jnp.concatenate([xr[h:], xi[h:]], 0).astype(BF16)
-    e = jnp.dot(left[2], even, preferred_element_type=F32)
-    o = jnp.dot(left[3], odd, preferred_element_type=F32)
+    e = dot(left[2], join([xr[:h], xi[:h]], 0).astype(BF16))
+    o = dot(left[3], join([xr[h:], xi[h:]], 0).astype(BF16))
     top, bottom = (e + o).astype(BF16), (e - o).astype(BF16)
-    middle = jnp.concatenate(
-        [
-            jnp.concatenate([top[:h], top[h:]], 1),
-            jnp.concatenate([bottom[:h], bottom[h:]], 1),
-        ],
-        0,
-    )
-    out = jnp.dot(middle, right[1], preferred_element_type=F32)
-    return out[:, : 2 * h], out[:, 2 * h :]
+
+    def columns(part):
+        lanes = slice(part * h, part * h + h)
+        return join(
+            [join([y[:h, lanes], y[h:, lanes]], 1) for y in (top, bottom)], 0
+        )
+
+    a, b = dot(columns(0), right[2]), dot(columns(1), right[3])
+    plus, minus = a + b, a - b
+    return join([plus[:, :h], minus[:, :h]], 1), join([plus[:, h:], minus[:, h:]], 1)
 
 
 def step_kernel(
     offsets, objects, probe_in, kernel_in, measured_in, left_in, right_in,
     out,
-    ext1, ext2, probe, turned, plain, kern, measured, left, right, held, pieces,
+    ext1, ext2, probe, turned, plain, kern, measured, left, right, held, pieces1, pieces2,
     strips, edge1, edge2, g_rows1, g_rows2, g_cols1, g_cols2, r_rows1, r_rows2, r_cols1, r_cols2,
     load_sems, send, recv,
 ):
@@ -105,7 +112,8 @@
     n_tiles = tile // LANES
     positions = measured.shape[0]
     extent = tile + 2 * HALO
-    gap = extent - width
+    pitch = width + HALO
+    pieces = (pieces1, pieces2)
     inner = pl.ds(HALO, tile)
     up_rows, down_rows = pl.ds(0, HALO), pl.ds(HALO + tile, HALO)
     first_rows, last_rows = pl.ds(HALO, HALO), pl.ds(tile, HALO)
@@ -153,7 +161,7 @@
     for t in range(width // LANES):
         load(measured_in.at[0, 0, :, :, pl.ds(t * LANES, LANES)], measured.at[:, t])
 
-    def exchange(phase, above, below, to_west, to_east, base, from_up, from_down, from_west, from_east):
+    def exchange(phase, to_west, to_east, base, from_west, from_east, above, below, from_up, from_down, between):
         main = pl.ds(base, tile)
         upper = pl.ds(0, HALO)
         lower = pl.ds(base + tile + base - HALO, HALO)
@@ -170,6 +178,8 @@
         ]
         copies = []
         for src, dst, k in moves:
+            if k == 0:
+                between()
             copy = pltpu.make_async_remote_copy(
                 src_ref=src, dst_ref=dst, send_sem=send.at[phase, k], recv_sem=recv.at[phase, k],
                 device_id=others[k], device_id_type=MESH,
@@ -187,17 +197,19 @@
         e = ext[s]
         return exchange(
             s,
+            strips.at[s, 0], strips.at[s, 1], 0, edge[s].at[0], edge[s].at[1],
             e.at[:, body_tiles, first_rows, :], e.at[:, body_tiles, last_rows, :],
-            strips.at[s, 0], strips.at[s, 1], 0,
             e.at[:, body_tiles, up_rows, :], e.at[:, body_tiles, down_rows, :],
-            edge[s].at[0], edge[s].at[1],
+            lambda: None,
         )
 
     def send_gradient(s):
         g, r = g_rows[s], r_rows[s]
         c, d = g_cols[s], r_cols[s]
+        gather_sides(s)
         return exchange(
-            2 + s, g.at[0], g.at[1], c.at[0], c.at[1], HALO, r.at[0], r.at[1], d.at[0], d.at[1]
+            2 + s, c.at[0], c.at[1], HALO, d.at[0], d.at[1],
+            g.at[0], g.at[1], r.at[0], r.at[1], lambda: gather_ends(s),
         )
 
     for copy in loads[:n_tiles]:
@@ -207,18 +219,33 @@
         strips[s, 0] = pack_low(ext[s][0, 1, inner, :], ext[s][1, 1, inner, :])
         strips[s, 1] = pack_high(ext[s][0, n_tiles, inner, :], ext[s][1, n_tiles, inner, :])
     pack(0)
+
+    def clear(i, carry):
+        rows = pl.ds(pl.multiple_of(i * pitch, HALO), HALO)
+        for ref in pieces:
+            ref[:, :, rows, :] = jnp.zeros((2, 3, HALO, LANES), F32)
+        return carry
+
+    lax.fori_loop(0, positions + 1, clear, 0)
     pl.semaphore_wait(barrier, neighbours)
     halo1 = send_halo(0)
 
     for copy in loads[n_tiles:]:
         copy.wait()
     pack(1)
-    def clear(i, carry):
-        rows = pl.ds(pl.multiple_of(i * extent, LANES), gap)
-        pieces[:, :, rows, :] = jnp.zeros((2, 3, gap, LANES), F32)
-        return carry
-
-    lax.fori_loop(0, positions + 1, clear, 0)
+    source = lax.broadcasted_iota(jnp.int32, (width, width), 0)
+    target = lane_index((width, width))
+    order = (source == jnp.where(target < h, 2 * target, 2 * target - (width - 1))).astype(F32)
+
+    def by_parity(whole):
+        return jnp.dot(
+            whole, order, precision=lax.Precision.HIGHEST, preferred_element_type=F32
+        )
+
+    for k in range(2):
+        whole = by_parity(join([plain[k, 0], plain[k, 1]], 1))
+        plain[k, 0] = whole[:, :h]
+        plain[k, 1] = whole[:, h:]
     for k in range(2):
         for parity in range(2):
             for t in range(width // LANES):
@@ -233,12 +260,16 @@
         return top, q, start - q * LANES
 
     def turn(p, carry):
+        whole = by_parity(join([measured[p, 0], measured[p, 1]], 1))
+        measured[p, 0] = whole[:, :h]
+        measured[p, 1] = whole[:, h:]
         r = where_of(p)[2]
         for k in range(2):
             turned[p, k] = pltpu.roll(probe[k], r, 1)
         return carry
 
     lax.fori_loop(0, positions, turn, 0)
+    halo2 = send_halo(1)
 
     def unpack_halo(s):
         both = edge[s][0]
@@ -255,16 +286,15 @@
         first = jnp.where(keep, ext[s][plane, q, rows, :], ext[s][plane, q + 2, rows, :])
         return jnp.concatenate([first, ext[s][plane, q + 1, rows, :]], 1)
 
-    def put(p, c, value):
-        rows = pl.ds(gap + p * extent, width)
+    def put(s, p, c, value):
+        rows = pl.ds(HALO + p * pitch, width)
         keep = lane_index((width, LANES)) >= where_of(p)[2]
         first = value[:, :LANES]
-        pieces[c, 0, rows, :] = jnp.where(keep, first, 0.0)
-        pieces[c, 1, rows, :] = value[:, LANES:]
-        pieces[c, 2, rows, :] = jnp.where(keep, 0.0, first)
+        pieces[s][c, 0, rows, :] = jnp.where(keep, first, 0.0)
+        pieces[s][c, 1, rows, :] = value[:, LANES:]
+        pieces[s][c, 2, rows, :] = jnp.where(keep, 0.0, first)
 
     finish(halo1)
-    halo2 = send_halo(1)
     unpack_halo(0)
 
     def stage_a(p, carry):
@@ -298,38 +328,39 @@
         factor = 1.0 - amplitude * lax.rsqrt(zr * zr + zi * zi + 1.0)
         gr, gi = inverse(zr * factor, zi * factor, left, right)
         sr, si = held[p, 0], held[p, 1]
-        put(p, 0, sr * gr + si * gi)
-        put(p, 1, sr * gi - si * gr)
-        o2r, o2i = window(1, 0, p), window(1, 1, p)
-        held[p, 0] = o2r * gr + o2i * gi
-        held[p, 1] = o2r * gi - o2i * gr
+        put(1, p, 0, sr * gr + si * gi)
+        put(1, p, 1, sr * gi - si * gr)
+        held[p, 0] = gr
+        held[p, 1] = gi
         return carry
 
     lax.fori_loop(0, positions, stage_b, 0, unroll=3)
 
-    def gather(t, row, count):
-        totals = [jnp.zeros((count, LANES), F32)] * 2
+    def gather(s, t, row):
+        totals = [jnp.zeros((HALO, LANES), F32)] * 2
         for p in range(positions):
             top, q, _ = spots[p]
-            inside = (t >= q) & (t <= q + 2)
+            ahead = row - top
+            inside = (t >= q) & (t <= q + 2) & (ahead > -HALO) & (ahead < width)
             slot = jnp.where(inside, t - q, 0)
-            rows = pl.ds(jnp.where(inside, gap + p * extent - top + row, 0), count)
-            totals = [totals[c] + pieces[c, slot, rows, :] for c in range(2)]
+            rows = pl.ds(jnp.where(inside, HALO + p * pitch + ahead, 0), HALO)
+            totals = [totals[c] + pieces[s][c, slot, rows, :] for c in range(2)]
         return totals
 
-    def gather_borders(s):
+    def gather_sides(s):
         def sides(i, carry):
             row = pl.multiple_of(i * HALO, HALO)
             rows = pl.ds(row, HALO)
-            g_cols[s][0, rows, :] = pack_high(*gather(0, row, HALO))
-            g_cols[s][1, rows, :] = pack_low(*gather(n_tiles + 1, row, HALO))
+            g_cols[s][0, rows, :] = pack_high(*gather(s, 0, row))
+            g_cols[s][1, rows, :] = pack_low(*gather(s, n_tiles + 1, row))
             return carry
 
         lax.fori_loop(0, extent // HALO, sides, 0)
 
+    def gather_ends(s):
         def ends(i, carry):
             for k in range(2):
-                totals = gather(1 + i, k * (HALO + tile), HALO)
+                totals = gather(s, 1 + i, k * (HALO + tile))
                 for c in range(2):
                     g_rows[s][k, c, i] = totals[c]
             return carry
@@ -340,7 +371,7 @@
         def chunk(i, carry):
             row = pl.multiple_of(i * HALO, HALO)
             for t in range(n_tiles):
-                totals = gather(t + 1, row + HALO, HALO)
+                totals = gather(s, t + 1, row + HALO)
                 for c in range(2):
                     out[2 * s + c, pl.ds(row, HALO), pl.ds(t * LANES, LANES)] = (
                         ext[s][c, t + 1, pl.ds(row + HALO, HALO), :] - RATE * totals[c]
@@ -369,25 +400,25 @@
             subtract(2 * s + 1, rows, n_tiles - 1, jnp.where(low, 0.0, both))
 
     spots = [where_of(p) for p in range(positions)]
-    gather_borders(1)
     sent2 = send_gradient(1)
-    gather_inner(1)
 
     def stage_c(p, carry):
-        ur, ui = forward(held[p, 0], held[p, 1], left, right)
+        gr, gi = held[p, 0], held[p, 1]
+        o2r, o2i = window(1, 0, p), window(1, 1, p)
+        ur, ui = forward(o2r * gr + o2i * gi, o2r * gi - o2i * gr, left, right)
         kr, kim = kern[0], kern[1]
         wr, wi = inverse(kr * ur + kim * ui, kr * ui - kim * ur, left, right)
         pr, pim = turned[p, 0], turned[p, 1]
-        put(p, 0, pr * wr + pim * wi)
-        put(p, 1, pr * wi - pim * wr)
+        put(0, p, 0, pr * wr + pim * wi)
+        put(0, p, 1, pr * wi - pim * wr)
         return carry
 
     lax.fori_loop(0, positions, stage_c, 0, unroll=3)
 
-    gather_borders(0)
+    sent1 = send_gradient(0)
+    gather_inner(1)
+    gather_inner(0)
     finish(sent2)
-    sent1 = send_gradient(0)
-    gather_inner(0)
     add_borders(1)
     finish(sent1)
     add_borders(0)
@@ -401,6 +432,7 @@
     positions = measured.shape[2]
     ext = pltpu.VMEM((2, n_tiles + 2, extent, LANES), F32)
     planes = pltpu.VMEM((positions, 2, width, width), F32)
+    pieces = pltpu.VMEM((2, 3, positions * (width + HALO) + HALO, LANES), F32)
     cols = pltpu.VMEM((2, extent, LANES), F32)
     rows = pltpu.VMEM((2, 2, n_tiles, HALO, LANES), F32)
     dma = pltpu.SemaphoreType.DMA
@@ -420,7 +452,8 @@
             pltpu.VMEM(left.shape, BF16),
             pltpu.VMEM(right.shape, BF16),
             planes,
-            pltpu.VMEM((2, 3, positions * extent + extent - width, LANES), F32),
+            pieces,
+            pieces,
             pltpu.VMEM((2, 2, tile, LANES), F32),
             cols, cols, rows, rows, cols, cols, rows, rows, cols, cols,
             dma((24,)), dma((4, 8)), dma((4, 8)),

time: 66.9 us -> 64.2 us (0.960)
  Pallas kernels: 64.4 us -> 61.8 us
    pallas_call x1, Pallas kernels: 64.4 us -> 61.8 us  [per_device(): pl.pallas_call(step_kernel, out_shape=pltpu.VMEM(objects.shape, F32), in_...]
where the time goes in v4:
time: 64.2 us; the launch traced here: 63.8 us
  Pallas kernels  61.8 us (96%)
  local copies, waits for them, and re-layouts  2.02 us (3%)
    pallas_call x1, Pallas kernels, per_device(): pl.pallas_call(step_kernel, out_shape=pltpu.VMEM(objects.shape, F32), in_...  61.8 us
    unnamed x1, local copies, waits for them, and re-layouts  2.02 us

profile of v4, /device:TPU:31, one launch (start us, length us, event | category | flops | bytes accessed | tf_op | source)
XLA Modules:
  0.0 63.8 jit_solution(18250245777321993643)
XLA Ops:
  0.0 61.8 %step.1 = f32[4,512,512]{2,1,0:T(8,128)S(1)} custom-call(s32[1,1,2,9]{3,2,1,0:T(2,128)} %bitcast.1, f32[4,512,512]{2,1,0:T(8,128)} %objects.1, f32[2,256,256]{2,1,0:T(8,128)} %probe_in.1, f32[2,256,256]{2,1,0:T(8,128)} %kernel_in.1, f32[1,1,9,256,256]{4,3,2,1,0:T(8,128)} %measured_in.1, bf16[4,256,256]{2,1,0:T(8,128)(2,1)} %constant.4.clone.left_in, ...), custom_call_target="tpu_custom_call" | custom-call | tf_op jit(solution)/shard_map/step/pallas_call | solution.py:439
  61.8 2.0 %copy.9 = f32[4,512,512]{2,1,0:T(8,128)} copy(f32[4,512,512]{2,1,0:T(8,128)S(1)} %step.1) | data formatting | bytes 8388608

commit v5 on v4

--- a/solution.py
+++ b/solution.py
@@ -132,17 +132,6 @@
               (north, west), (north, east), (south, west), (south, east)]
     here = [has_n, has_s, has_w, has_e, has_n & has_w, has_n & has_e, has_s & has_w, has_s & has_e]
     opposite = [1, 0, 3, 2, 7, 6, 5, 4]
-    for ref in (r_rows1, r_rows2, r_cols1, r_cols2):
-        ref[...] = jnp.zeros_like(ref)
-    barrier = pltpu.get_barrier_semaphore()
-    neighbours = 0
-    for other, there in zip(others, here):
-        neighbours = neighbours + there.astype(jnp.int32)
-
-        @pl.when(there)
-        def _():
-            pl.semaphore_signal(barrier, inc=1, device_id=other, device_id_type=MESH)
-
     loads = []
 
     def load(src, dst):
@@ -160,6 +149,17 @@
     load(right_in, right)
     for t in range(width // LANES):
         load(measured_in.at[0, 0, :, :, pl.ds(t * LANES, LANES)], measured.at[:, t])
+
+    for ref in (r_rows1, r_rows2, r_cols1, r_cols2):
+        ref[...] = jnp.zeros_like(ref)
+    barrier = pltpu.get_barrier_semaphore()
+    neighbours = 0
+    for other, there in zip(others, here):
+        neighbours = neighbours + there.astype(jnp.int32)
+
+        @pl.when(there)
+        def _():
+            pl.semaphore_signal(barrier, inc=1, device_id=other, device_id_type=MESH)
 
     def exchange(phase, to_west, to_east, base, from_west, from_east, above, below, from_up, from_down, between):
         main = pl.ds(base, tile)
@@ -193,14 +193,14 @@
             pl.when(here[k])(copy.wait_send)
             pl.when(here[opposite[k]])(copy.wait_recv)
 
-    def send_halo(s):
+    def send_halo(s, between):
         e = ext[s]
         return exchange(
             s,
             strips.at[s, 0], strips.at[s, 1], 0, edge[s].at[0], edge[s].at[1],
             e.at[:, body_tiles, first_rows, :], e.at[:, body_tiles, last_rows, :],
             e.at[:, body_tiles, up_rows, :], e.at[:, body_tiles, down_rows, :],
-            lambda: None,
+            between,
         )
 
     def send_gradient(s):
@@ -228,7 +228,7 @@
 
     lax.fori_loop(0, positions + 1, clear, 0)
     pl.semaphore_wait(barrier, neighbours)
-    halo1 = send_halo(0)
+    halo1 = send_halo(0, lambda: None)
 
     for copy in loads[n_tiles:]:
         copy.wait()
@@ -269,8 +269,6 @@
         return carry
 
     lax.fori_loop(0, positions, turn, 0)
-    halo2 = send_halo(1)
-
     def unpack_halo(s):
         both = edge[s][0]
         ext[s][0, 0] = pltpu.roll(both, HALF, 1)
@@ -294,7 +292,7 @@
         pieces[s][c, 1, rows, :] = value[:, LANES:]
         pieces[s][c, 2, rows, :] = jnp.where(keep, 0.0, first)
 
-    finish(halo1)
+    halo2 = send_halo(1, lambda: finish(halo1))
     unpack_halo(0)
 
     def stage_a(p, carry):
@@ -336,31 +334,42 @@
 
     lax.fori_loop(0, positions, stage_b, 0, unroll=3)
 
-    def gather(s, t, row):
+    far = 8 * extent
+
+    def places(t):
+        found = []
+        for top, q, _ in spots:
+            ahead = t - q
+            near = (ahead >= 0) & (ahead <= 2)
+            found.append((jnp.where(near, top, far), jnp.where(near, ahead, 0)))
+        return found
+
+    def gather(s, found, row):
         totals = [jnp.zeros((HALO, LANES), F32)] * 2
-        for p in range(positions):
-            top, q, _ = spots[p]
+        for p, (top, slot) in enumerate(found):
             ahead = row - top
-            inside = (t >= q) & (t <= q + 2) & (ahead > -HALO) & (ahead < width)
-            slot = jnp.where(inside, t - q, 0)
-            rows = pl.ds(jnp.where(inside, HALO + p * pitch + ahead, 0), HALO)
+            inside = (ahead > -HALO) & (ahead < width)
+            rows = pl.ds(jnp.where(inside, ahead + (HALO + p * pitch), 0), HALO)
             totals = [totals[c] + pieces[s][c, slot, rows, :] for c in range(2)]
         return totals
 
     def gather_sides(s):
+        first, last = places(0), places(n_tiles + 1)
+
         def sides(i, carry):
             row = pl.multiple_of(i * HALO, HALO)
             rows = pl.ds(row, HALO)
-            g_cols[s][0, rows, :] = pack_high(*gather(s, 0, row))
-            g_cols[s][1, rows, :] = pack_low(*gather(s, n_tiles + 1, row))
+            g_cols[s][0, rows, :] = pack_high(*gather(s, first, row))
+            g_cols[s][1, rows, :] = pack_low(*gather(s, last, row))
             return carry
 
         lax.fori_loop(0, extent // HALO, sides, 0)
 
     def gather_ends(s):
         def ends(i, carry):
+            found = places(1 + i)
             for k in range(2):
-                totals = gather(s, 1 + i, k * (HALO + tile))
+                totals = gather(s, found, k * (HALO + tile))
                 for c in range(2):
                     g_rows[s][k, c, i] = totals[c]
             return carry
@@ -371,7 +380,7 @@
         def chunk(i, carry):
             row = pl.multiple_of(i * HALO, HALO)
             for t in range(n_tiles):
-                totals = gather(s, t + 1, row + HALO)
+                totals = gather(s, places(t + 1), row + HALO)
                 for c in range(2):
                     out[2 * s + c, pl.ds(row, HALO), pl.ds(t * LANES, LANES)] = (
                         ext[s][c, t + 1, pl.ds(row + HALO, HALO), :] - RATE * totals[c]

time: 64.2 us -> 63.6 us (level)
  no operation moved by 1% of the time
where the time goes in v5:
time: 63.6 us; the launch traced here: 63.2 us
  Pallas kernels  61.2 us (96%)
  local copies, waits for them, and re-layouts  2.02 us (3%)
    pallas_call x1, Pallas kernels, per_device(): pl.pallas_call(step_kernel, out_shape=pltpu.VMEM(objects.shape, F32), in_...  61.2 us
    unnamed x1, local copies, waits for them, and re-layouts  2.02 us

profile of v5, /device:TPU:31, one launch (start us, length us, event | category | flops | bytes accessed | tf_op | source)
XLA Modules:
  0.0 63.2 jit_solution(6458044613588334252)
XLA Ops:
  0.0 61.2 %step.1 = f32[4,512,512]{2,1,0:T(8,128)S(1)} custom-call(s32[1,1,2,9]{3,2,1,0:T(2,128)} %bitcast.1, f32[4,512,512]{2,1,0:T(8,128)} %objects.1, f32[2,256,256]{2,1,0:T(8,128)} %probe_in.1, f32[2,256,256]{2,1,0:T(8,128)} %kernel_in.1, f32[1,1,9,256,256]{4,3,2,1,0:T(8,128)} %measured_in.1, bf16[4,256,256]{2,1,0:T(8,128)(2,1)} %constant.4.clone.left_in, ...), custom_call_target="tpu_custom_call" | custom-call | tf_op jit(solution)/shard_map/step/pallas_call | solution.py:448
  61.2 2.0 %copy.9 = f32[4,512,512]{2,1,0:T(8,128)} copy(f32[4,512,512]{2,1,0:T(8,128)S(1)} %step.1) | data formatting | bytes 8388608
